TPU v7x, 16 devices: a 4x2x1 block of a 4x4x8 slice. The times are simulated.
16 devices in a mesh: dp: 2 (over y, z), dcp: 8 (over x, core).
Axes of the slice: x: 4, y: 2, z: 1, core: 2. Of those that a mesh axis runs over, the one named last changes fastest.
The devices are a block of a 4x4x8 slice.
Arguments:
- q_abs: bfloat16 [128, 128, 576], P('dp', 'dcp'), parts along dimension 0
- cache: bfloat16 [128, 8192, 576], P('dp', 'dcp'), parts along dimension 0
- lengths: int32 [128], P('dp'), parts along dimension 0
Outputs:
- output: bfloat16 [128, 128, 512], P('dp', 'dcp'), parts along dimension 0
There are 2 independent parts. A program takes and returns all parts, laid end to end along the dimension named above; each array names one.
All inputs are finite; a program needn't handle non-finite values.
Results may differ from a plain program's by a relative error of at most 0.00748833.
Values are sent between devices in bfloat16 or wider.
A program may use at most 768 MiB of HBM per device.

v0:
```python
import jax
import jax.numpy as jnp
from jax import lax
from jax.sharding import PartitionSpec as P

ROPE = 64
SCALE = 192 ** -0.5


def partial_attention(q, blk, valid, lat):
    s = jnp.einsum('bhk,btk->bht', q, blk, preferred_element_type=jnp.float32) * SCALE
    s = jnp.where(valid[:, None, :], s, -jnp.inf)
    m = jnp.max(s, axis=2)
    m0 = jnp.where(jnp.isfinite(m), m, 0.0)
    p = jnp.exp(s - m0[:, :, None])
    l = jnp.sum(p, axis=2)
    pv = jnp.einsum('bht,btc->bhc', p.astype(jnp.bfloat16), blk[:, :, :lat], preferred_element_type=jnp.float32)
    has = l > 0.0
    l1 = jnp.where(has, l, 1.0)
    od = (pv / l1[:, :, None]).astype(jnp.bfloat16)
    lse = jnp.where(has, m0 + jnp.log(l1), -jnp.inf)
    return od, lse


def merge(od, lse, axis):
    mx = jnp.max(lse, axis=axis, keepdims=True)
    wt = jnp.exp(lse - mx)
    wt = wt / jnp.sum(wt, axis=axis, keepdims=True)
    return jnp.sum(wt[..., None] * od.astype(jnp.float32), axis=axis).astype(jnp.bfloat16)


def solution(mesh):
    n = mesh.shape['dcp']

    def local(q, cache, lengths):
        d = lax.axis_index('dcp')
        b, sl, wd = cache.shape
        lat = wd - ROPE
        qa = lax.all_gather(q, 'dcp', axis=1, tiled=True)
        pos = d * sl + jnp.arange(sl)
        valid = pos[None, :] < lengths[:, None]
        od, lse = partial_attention(qa, cache, valid, lat)
        h = od.shape[1]
        od = od.reshape(b, n, h // n, lat)
        lse = lse.reshape(b, n, h // n)
        od = lax.all_to_all(od, 'dcp', 1, 1, tiled=True)
        lse = lax.all_to_all(lse, 'dcp', 1, 1, tiled=True)
        return merge(od, lse, 1)

    return jax.shard_map(local, mesh=mesh, in_specs=(P('dp', 'dcp', None), P('dp', 'dcp', None), P('dp')), out_specs=P('dp', 'dcp', None), check_vma=False)
```

profile of v0, /device:TPU:112, one launch (start us, length us, event | category | flops | bytes accessed | tf_op | source)
XLA Modules:
  0.0 286.9 jit_solution(17279185159750049099)
XLA Ops:
  6.5 0.0 all-gather.2.cloned.1.call-start
  6.6 0.7 all-gather.2.cloned.1.call-update
  7.3 0.8 broadcast_compare_fusion
  8.1 58.1 %all-gather.2.cloned.1.call-done = bf16[64,128,576]{2,1,0:T(8,128)(2,1)} async-done(((bf16[64,16,576]{2,1,0:T(8,128)(2,1)}), bf16[64,128,576]{2,1,0:T(8,128)(2,1)}) %all-gather.2.cloned.1.call-update) | async-done | bytes 9437200 | tf_op jit(solution)/shard_map/all_gather | solution.py:39
  66.2 41.4 %fusion.2 = (f32[64,128]{1,0:T(8,128)S(1)}, f32[64,128,1024]{2,1,0:T(8,128)}) fusion(pred[64,1024]{1,0:T(8,128)(4,1)S(1)} %broadcast_compare_fusion, bf16[64,128,576]{2,1,0:T(8,128)(2,1)} %all-gather.2.cloned.1.call-done, bf16[64,1024,576]{1,2,0:T(8,128)(2,1)} %param.4), kind=kOutput, calls=%fused_computation.4 | convolution fusion | flops 9688834048 | bytes 118587392 | tf_op jit(solution)/shard_map/bhk,btk->bht/dot_general | solution.py:11
  107.6 0.1 copy.10
  107.7 14.9 %fusion.4 = f32[64,128]{1,0:T(8,128)S(1)} fusion(f32[64,128,1024]{2,1,0:T(8,128)} %get-tuple-element.6, f32[64,128]{1,0:T(8,128)S(1)} %is-finite_select_fusion.1, pred[64,1024]{1,0:T(8,128)(4,1)S(1)} %broadcast_compare_fusion), kind=kLoop, calls=%fused_computation.6 | loop fusion | flops 33546240 | bytes 33685504 | tf_op jit(solution)/shard_map/reduce_sum | solution.py:16
  122.6 0.1 copy.9
  122.7 0.7 reshape.45
  123.5 3.5 %all-to-all-start = ((f32[8,1,1024]{2,1,0:T(1,128)}), f32[8,1,1024]{2,1,0:T(1,128)S(1)}, u32[]{:S(2)}, u32[]{:S(2)}) async-start(f32[8,1,1024]{2,1,0:T(1,128)} %reshape.45), calls=%async_computation | async-start | bytes 65536 | tf_op jit(solution)/shard_map/all_to_all | solution.py:47
  127.0 39.2 %divide_convert_fusion = bf16[64,128,512]{2,1,0:T(8,128)(2,1)} fusion(f32[64,128]{1,0:T(8,128)S(1)} %compare_select_fusion, bf16[64,1024,576]{1,2,0:T(8,128)(2,1)} %param.4, f32[64,128,1024]{2,1,0:T(8,128)} %get-tuple-element.6, f32[64,128]{1,0:T(8,128)S(1)} %is-finite_select_fusion.1, pred[64,1024]{1,0:T(8,128)(4,1)S(1)} %broadcast_compare_fusion), kind=kOutput, calls=%fused_computation.8 | convolution fusion | flops 8631877632 | bytes 109182976 | tf_op jit(solution)/shard_map/bht,btc->bhc/dot_general | solution.py:17
  166.3 8.0 %copy.13 = bf16[64,8,16,512]{3,2,0,1:T(8,128)(2,1)} copy(bf16[64,8,16,512]{3,2,1,0:T(8,128)(2,1)} %bitcast.11) | data formatting | bytes 16777216 | tf_op jit(solution)/shard_map/reshape | solution.py:44
  174.3 0.0 all-to-all-done
  174.3 5.2 %all-to-all-start.1 = ((bf16[64,8,16,512]{3,2,0,1:T(8,128)(2,1)}), bf16[64,8,16,512]{3,2,0,1:T(8,128)(2,1)}, u32[]{:S(2)}, u32[]{:S(2)}) async-start(bf16[64,8,16,512]{3,2,0,1:T(8,128)(2,1)} %copy.13), calls=%async_computation.1 | async-start | bytes 16777216 | tf_op jit(solution)/shard_map/all_to_all | solution.py:46
  179.5 0.5 broadcast.38
  180.0 0.7 reduce
  180.7 0.1 reshape.46
  180.9 0.1 copy.11
  181.0 92.9 %all-to-all-done.1 = bf16[64,8,16,512]{3,2,0,1:T(8,128)(2,1)} async-done(((bf16[64,8,16,512]{3,2,0,1:T(8,128)(2,1)}), bf16[64,8,16,512]{3,2,0,1:T(8,128)(2,1)}, u32[]{:S(2)}, u32[]{:S(2)}) %all-to-all-start.1) | async-done | bytes 8388640 | tf_op jit(solution)/shard_map/all_to_all | solution.py:46
  273.9 6.2 %multiply_reduce_fusion = bf16[64,16,512]{2,1,0:T(8,128)(2,1)} fusion(bf16[64,8,16,512]{3,2,0,1:T(8,128)(2,1)} %all-to-all-done.1, f32[64,8,16]{2,0,1:T(8,128)S(1)} %copy.11), kind=kLoop, calls=%fused_computation.7 | loop fusion | flops 12058624 | bytes 9469952 | tf_op jit(solution)/shard_map/reduce_sum | solution.py:29
  (7 shorter events, 0.1 us)
Async XLA Ops:
  6.5 59.6 %all-gather.2.cloned.1.call-start = ((), (), s32[]{:S(2)}) async-start(), calls=%async_computation.2 | async-start | bytes 11796480 | tf_op jit(solution)/shard_map/all_gather | solution.py:39
  123.5 50.8 %all-to-all-start = ((f32[8,1,1024]{2,1,0:T(1,128)}), f32[8,1,1024]{2,1,0:T(1,128)S(1)}, u32[]{:S(2)}, u32[]{:S(2)}) async-start(f32[8,1,1024]{2,1,0:T(1,128)} %reshape.45), calls=%async_computation | async-start | bytes 65536 | tf_op jit(solution)/shard_map/all_to_all | solution.py:47
  174.3 99.6 %all-to-all-start.1 = ((bf16[64,8,16,512]{3,2,0,1:T(8,128)(2,1)}), bf16[64,8,16,512]{3,2,0,1:T(8,128)(2,1)}, u32[]{:S(2)}, u32[]{:S(2)}) async-start(bf16[64,8,16,512]{3,2,0,1:T(8,128)(2,1)} %copy.13), calls=%async_computation.1 | async-start | bytes 16777216 | tf_op jit(solution)/shard_map/all_to_all | solution.py:46
Sparse Core Ops, SparseCore 0:
  8.9 57.1 all-gather.1
where the time goes:
time: 287 us
  waiting for transfers between devices  152 us (53%)
  matrix products  80.7 us (28%)
  other arithmetic  22.7 us (8%)
  between operations  13.5 us (5%)
  local copies, waits for them, and re-layouts  9.61 us (3%)
  starting transfers between devices  8.77 us (3%)
    all_to_all x1, waiting for transfers between devices, local(): od = lax.all_to_all(od, 'dcp', 1, 1, tiled=True)  92.9 us
    all_gather x1, waiting for transfers between devices, local(): qa = lax.all_gather(q, 'dcp', axis=1, tiled=True)  58.1 us
    dot_general x1, matrix products, partial_attention(): jnp.einsum('bhk,btk->bht', q, blk, preferred_element_type=jnp.float32)  41.4 us
    dot_general x1, matrix products, partial_attention(): jnp.einsum('bht,btc->bhc', p.astype(jnp.bfloat16), blk[:, :, :lat], prefe...  39.2 us
    reduce_sum x1, other arithmetic, partial_attention(): l = jnp.sum(p, axis=2)  14.9 us
    reshape x1, local copies, waits for them, and re-layouts, local(): od = od.reshape(b, n, h // n, lat)  8 us
    reduce_sum x1, other arithmetic, merge(): jnp.sum(wt[..., None] * od.astype(jnp.float32), axis=axis)  6.18 us
  transfers between devices with their start and end apart: 3, of which 2 were waited for; matrix products, arithmetic and copies ran while one was open for 17% of the time, Pallas kernels for 0%

commit v1 on v0

v1 whole, which is shorter than its diff:
```python
import functools

import jax
import jax.numpy as jnp
from jax import lax
from jax.experimental import pallas as pl
from jax.experimental.pallas import tpu as pltpu
from jax.sharding import PartitionSpec as P

ROPE = 64
SCALE = 192 ** -0.5
CORES = 2
CHUNK = 8
PAIRS = 4
LAG_R = 1
LAG_F = 2

MESH = pl.DeviceIdType.MESH
F32 = jnp.float32
BF16 = jnp.bfloat16
VIA, DIRECT, MINE, PASS, SUM = 0, 2, 4, 5, 6


def weights(stats):
    top = functools.reduce(jnp.maximum, stats)
    top = jnp.maximum(top, jnp.finfo(F32).min)
    w = [jnp.exp(t - top) for t in stats]
    total = functools.reduce(jnp.add, w)
    inv = 1.0 / jnp.maximum(total, 1.0)
    return [x * inv for x in w], top + jnp.log(total)


def kernel(n, len_ref, q_ref, ct_ref, o_ref, qraw, qg, od, st, inc, ins, lg, rs, rss, obuf, cbuf,
           raw_sem, cache_sem, out_sem, q_send, q_recv, o_send, o_recv, t_send, t_recv):
    chips = n // CORES
    nb, hl, wd = q_ref.shape
    lat = wd - ROPE
    heads = n * hl
    sl = ct_ref.shape[2]
    nc = nb // CHUNK
    half = CHUNK // 2
    npair = nb // 2

    me = lax.axis_index('dcp')
    x = me // CORES
    k = me % CORES
    partner = x * CORES + (1 - k)

    def dev(step, core):
        return ((x + step + chips) % chips) * CORES + core

    def cache_copies(pair, par):
        slot = (pair % PAIRS) * 2 + par
        b = pair * 2 + par
        if par == 0:
            return [pltpu.make_async_copy(ct_ref.at[b], cbuf.at[slot, pl.ds(0, wd)], cache_sem.at[slot, 0])]
        return [
            pltpu.make_async_copy(ct_ref.at[b, pl.ds(0, lat)], cbuf.at[slot, pl.ds(0, lat)], cache_sem.at[slot, 0]),
            pltpu.make_async_copy(ct_ref.at[b, pl.ds(lat, ROPE)], cbuf.at[slot, pl.ds(wd, ROPE)], cache_sem.at[slot, 1]),
        ]

    def fetch(pair):
        for par in range(2):
            for cp in cache_copies(pair, par):
                cp.start()

    raw = pltpu.make_async_copy(q_ref, qraw, raw_sem)
    raw.start()

    barrier = pltpu.get_barrier_semaphore()
    peers = [partner, dev(1, 0), dev(1, 1), dev(-1, 0), dev(-1, 1)]
    for peer in peers:
        pl.semaphore_signal(barrier, inc=1, device_id={'dcp': peer}, device_id_type=MESH)

    for g in range(PAIRS):
        cbuf[2 * g, pl.ds(wd, ROPE), :] = jnp.zeros((ROPE, sl), BF16)
        cbuf[2 * g + 1, pl.ds(lat, ROPE), :] = jnp.zeros((ROPE, sl), BF16)
    raw.wait()

    def pack(g, _):
        for par in range(2):
            qg[me, g, :, pl.ds(par * lat, lat)] = qraw[2 * g + par, :, pl.ds(0, lat)]
        r0 = qraw[2 * g, :, pl.ds(lat, ROPE)]
        r1 = qraw[2 * g + 1, :, pl.ds(lat, ROPE)]
        qg[me, g, :, pl.ds(2 * lat, 2 * ROPE)] = jnp.concatenate([r0, r1], axis=1)
        return 0

    lax.fori_loop(0, npair, pack, 0)
    for g in range(PAIRS):
        fetch(g)
    pl.semaphore_wait(barrier, len(peers))

    def q_copy(kind, src, c, to):
        part = qg.at[src, pl.ds(c * half, half)]
        return pltpu.make_async_remote_copy(
            src_ref=part, dst_ref=part, send_sem=q_send.at[kind, c], recv_sem=q_recv.at[kind, c],
            device_id={'dcp': to}, device_id_type=MESH)

    def q_wait(kind, src, c):
        q_copy(kind, src, c, me).wait_recv()

    def sign(c):
        return 1 - 2 * (c % 2)

    def q0(c, _):
        q_copy(0, me, c, dev(1, k)).start()
        q_copy(1, me, c, dev(-1, k)).start()
        q_copy(2, me, c, partner).start()
        return 0

    lax.fori_loop(0, nc, q0, 0)

    def q1(c, _):
        way = -sign(c)
        q_wait(0, dev(-1, k), c)
        q_copy(3, dev(-1, k), c, partner).start()
        q_wait(1, dev(1, k), c)
        q_copy(4, dev(1, k), c, partner).start()
        q_copy(5, dev(-way, k), c, dev(way, k)).start()
        return 0

    lax.fori_loop(0, nc, q1, 0)

    def q2(c):
        q_wait(5, dev(2, k), c)
        q_copy(6, dev(2, k), c, partner).start()

    def q3(c):
        q_wait(2, partner, c)
        q_wait(3, dev(-1, 1 - k), c)
        q_wait(4, dev(1, 1 - k), c)
        q_wait(6, dev(2, 1 - k), c)

    lane = lax.broadcasted_iota(jnp.int32, (heads, 128), 1)
    where_t = lax.broadcasted_iota(jnp.int32, (1, sl), 1)
    base = me * sl

    def attend(c):
        def pair_step(i, stat):
            g = c * half + i
            for par in range(2):
                b = g * 2 + par
                slot = (g % PAIRS) * 2 + par
                for cp in cache_copies(g, par):
                    cp.wait()
                qa = qg[:, g, :, pl.ds(par * lat, lat)].reshape(heads, lat)
                qr = qg[:, g, :, pl.ds(2 * lat, 2 * ROPE)].reshape(heads, 2 * ROPE)
                s = jnp.dot(qa, cbuf[slot, pl.ds(0, lat), :], preferred_element_type=F32)
                s = s + jnp.dot(qr, cbuf[slot, pl.ds(lat, 2 * ROPE), :], preferred_element_type=F32)
                s = jnp.where(where_t < len_ref[b] - base, s * SCALE, -jnp.inf)
                m = jnp.maximum(jnp.max(s, axis=1, keepdims=True), jnp.finfo(F32).min)
                p = jnp.exp(s - m)
                l = jnp.sum(p, axis=1, keepdims=True)
                pv = lax.dot_general(p.astype(BF16), cbuf[slot, pl.ds(0, lat), :], (((1,), (1,)), ((), ())),
                                     preferred_element_type=F32)
                o = (pv * (1.0 / jnp.maximum(l, 1.0))).astype(BF16)
                od[:, b, :, :] = o.reshape(n, hl, lat)
                stat = jnp.where(lane == i * 2 + par, m + jnp.log(l), stat)

            @pl.when(g + PAIRS < npair)
            def _():
                fetch(g + PAIRS)

            return stat

        stat = lax.fori_loop(0, half, pair_step, jnp.full((heads, 128), -jnp.inf, F32))
        st[:, c, :, :] = stat.reshape(n, hl, 128)

    def rows(c):
        return pl.ds(c * CHUNK, CHUNK)

    def o_copies(c, head, slot_s, slot_r, to):
        return [
            pltpu.make_async_remote_copy(
                src_ref=od.at[head, rows(c)], dst_ref=inc.at[slot_r, rows(c)],
                send_sem=o_send.at[slot_s, c], recv_sem=o_recv.at[slot_r, c],
                device_id={'dcp': to}, device_id_type=MESH),
            pltpu.make_async_remote_copy(
                src_ref=st.at[head, c], dst_ref=ins.at[slot_r, c],
                send_sem=t_send.at[slot_s, c], recv_sem=t_recv.at[slot_r, c],
                device_id={'dcp': to}, device_id_type=MESH),
        ]

    def sends(c):
        way = sign(c)
        out = []
        for kk in range(CORES):
            out += o_copies(c, dev(2, kk), VIA + kk, VIA + k, dev(way, kk))
        out += o_copies(c, dev(way, 1 - k), PASS, PASS, partner)
        out += o_copies(c, partner, MINE, MINE, partner)
        for kk in range(CORES):
            out += o_copies(c, dev(-way, kk), DIRECT + kk, DIRECT + k, dev(-way, kk))
        return out

    def sum_copies(c):
        to = dev(sign(c), k)
        return [
            pltpu.make_async_remote_copy(
                src_ref=rs.at[rows(c)], dst_ref=lg.at[rows(c)], send_sem=o_send.at[SUM, c], recv_sem=o_recv.at[SUM, c],
                device_id={'dcp': to}, device_id_type=MESH),
            pltpu.make_async_remote_copy(
                src_ref=rss.at[c], dst_ref=ins.at[SUM, c], send_sem=t_send.at[SUM, c], recv_sem=t_recv.at[SUM, c],
                device_id={'dcp': to}, device_id_type=MESH),
        ]

    def o_wait(c, slot):
        for cp in o_copies(c, me, slot, slot, me):
            cp.wait_recv()

    def relay(c):
        for slot in (PASS, VIA, VIA + 1):
            o_wait(c, slot)
        mine = dev(sign(c), k)
        w, lse = weights([st[mine, c], ins[PASS, c], ins[VIA, c], ins[VIA + 1, c]])
        for i in range(CHUNK):
            b = c * CHUNK + i
            acc = w[0][:, i:i + 1] * od[mine, b].astype(F32)
            for j, slot in ((1, PASS), (2, VIA), (3, VIA + 1)):
                acc = acc + w[j][:, i:i + 1] * inc[slot, b].astype(F32)
            rs[b] = acc
        rss[c] = lse
        for cp in sum_copies(c):
            cp.start()

    def out_copy(c):
        return pltpu.make_async_copy(obuf.at[rows(c)], o_ref.at[rows(c)], out_sem.at[c])

    def merge(c):
        for slot in (MINE, DIRECT, DIRECT + 1):
            o_wait(c, slot)
        for cp in sum_copies(c):
            cp.wait_recv()
        w, _ = weights([st[me, c], ins[MINE, c], ins[DIRECT, c], ins[DIRECT + 1, c], ins[SUM, c]])
        for i in range(CHUNK):
            b = c * CHUNK + i
            acc = w[0][:, i:i + 1] * od[me, b].astype(F32)
            for j, slot in ((1, MINE), (2, DIRECT), (3, DIRECT + 1)):
                acc = acc + w[j][:, i:i + 1] * inc[slot, b].astype(F32)
            acc = acc + w[4][:, i:i + 1] * lg[b]
            obuf[b] = acc.astype(BF16)
        out_copy(c).start()

    q2(0)

    def step(t, _):
        @pl.when(t < nc)
        def _():
            @pl.when(t + 1 < nc)
            def _():
                q2(t + 1)

            q3(t)
            attend(t)
            for cp in sends(t):
                cp.start()

        @pl.when(jnp.logical_and(t >= LAG_R, t < nc + LAG_R))
        def _():
            relay(t - LAG_R)

        @pl.when(t >= LAG_F)
        def _():
            merge(t - LAG_F)

        return 0

    lax.fori_loop(0, nc + LAG_F, step, 0)

    def drain(c, _):
        for kind in range(7):
            q_copy(kind, me, c, me).wait_send()
        for cp in sends(c) + sum_copies(c):
            cp.wait_send()
        out_copy(c).wait()
        return 0

    lax.fori_loop(0, nc, drain, 0)


def solution(mesh):
    n = mesh.shape['dcp']

    def local(q, cache, lengths):
        nb, hl, wd = q.shape
        sl = cache.shape[1]
        lat = wd - ROPE
        nc = nb // CHUNK
        anyspace = pl.BlockSpec(memory_space=pl.ANY)
        dma = pltpu.SemaphoreType.DMA
        return pl.pallas_call(
            functools.partial(kernel, n),
            out_shape=jax.ShapeDtypeStruct((nb, hl, lat), BF16),
            in_specs=[pl.BlockSpec(memory_space=pltpu.SMEM), anyspace, anyspace],
            out_specs=anyspace,
            scratch_shapes=[
                pltpu.VMEM((nb, hl, wd), BF16),
                pltpu.VMEM((n, nb // 2, hl, 2 * wd), BF16),
                pltpu.VMEM((n, nb, hl, lat), BF16),
                pltpu.VMEM((n, nc, hl, 128), F32),
                pltpu.VMEM((6, nb, hl, lat), BF16),
                pltpu.VMEM((7, nc, hl, 128), F32),
                pltpu.VMEM((nb, hl, lat), F32),
                pltpu.VMEM((nb, hl, lat), F32),
                pltpu.VMEM((nc, hl, 128), F32),
                pltpu.VMEM((nb, hl, lat), BF16),
                pltpu.VMEM((2 * PAIRS, wd + ROPE, sl), BF16),
                dma,
                dma((2 * PAIRS, 2)),
                dma((nc,)),
                dma((7, nc)),
                dma((7, nc)),
                dma((7, nc)),
                dma((7, nc)),
                dma((7, nc)),
                dma((7, nc)),
            ],
            compiler_params=pltpu.CompilerParams(
                collective_id=0, has_side_effects=True, vmem_limit_bytes=63 * 1024 * 1024),
            name='mla_decode',
        )(lengths, q, jnp.swapaxes(cache, 1, 2))

    return jax.shard_map(local, mesh=mesh, in_specs=(P('dp', 'dcp', None), P('dp', 'dcp', None), P('dp')),
                         out_specs=P('dp', 'dcp', None), check_vma=False)
```

time: 287 us -> 135 us (0.47)
  waiting for transfers between devices: 152 us -> 0 us
  Pallas kernels: 0 us -> 131 us
  matrix products: 80.7 us -> 0 us
  other arithmetic: 22.7 us -> 0 us
  between operations: 13.5 us -> 0.01 us
  starting transfers between devices: 8.77 us -> 0 us
  local copies, waits for them, and re-layouts: 9.61 us -> 2.26 us
    pallas_call x0 -> x1, Pallas kernels: none -> 131 us  [local(): pl.pallas_call(functools.partial(kernel, n), out_shape=jax.ShapeDtypeStru...]
    all_to_all x2 -> x0, waiting for transfers between devices: 92.9 us -> none  [the longest x1 92.9 us: local(): od = lax.all_to_all(od, 'dcp', 1, 1, tiled=True)]
    dot_general x2 -> x0, matrix products: 80.7 us -> none  [the longest x1 41.4 us: partial_attention(): jnp.einsum('bhk,btk->bht', q, blk, preferred_element_type=jnp.float32)]
    all_gather x1 -> x0, waiting for transfers between devices: 58.1 us -> none  [local(): qa = lax.all_gather(q, 'dcp', axis=1, tiled=True)]
    reduce_sum x3 -> x0, other arithmetic: 21.1 us -> none  [the longest x1 14.9 us: partial_attention(): l = jnp.sum(p, axis=2)]
    all_to_all x2 -> x0, starting transfers between devices: 8.77 us -> none  [the longest x1 5.22 us: local(): od = lax.all_to_all(od, 'dcp', 1, 1, tiled=True)]
    reshape x1 -> x0, local copies, waits for them, and re-layouts: 8 us -> none  [local(): od = od.reshape(b, n, h // n, lat)]
  transfers between devices with their start and end apart: 3 -> 0, of which waited for: 2 -> 0; matrix products, arithmetic and copies ran while one was open for 17% -> 0% of each run, Pallas kernels for 0% -> 0%
where the time goes in v1:
time: 135 us; the launch traced here: 134 us
  Pallas kernels  131 us (97%)
  local copies, waits for them, and re-layouts  2.26 us (2%)
    pallas_call x1, Pallas kernels, local(): pl.pallas_call(functools.partial(kernel, n), out_shape=jax.ShapeDtypeStru...  131 us

profile of v1, /device:TPU:112, one launch (start us, length us, event | category | flops | bytes accessed | tf_op | source)
XLA Modules:
  0.0 133.7 jit_solution(10365725530484478345)
XLA Ops:
  0.0 131.4 %mla_decode.1 = bf16[64,16,512]{2,1,0:T(8,128)(2,1)} custom-call(s32[64]{0:T(128)} %len_ref.1, bf16[64,16,576]{2,1,0:T(8,128)(2,1)} %q_ref.1, bf16[64,576,1024]{2,1,0:T(8,128)(2,1)} %bitcast.ct_ref), custom_call_target="tpu_custom_call" | custom-call | tf_op jit(solution)/shard_map/mla_decode/pallas_call | solution.py:290
  131.4 2.3 %copy.5 = bf16[64,16,512]{2,1,0:T(8,128)(2,1)} copy(bf16[64,16,512]{2,1,0:T(8,128)(2,1)} %mla_decode.1) | data formatting | bytes 2097152

commit v2 on v1

--- a/solution.py
+++ b/solution.py
@@ -12,8 +12,8 @@
 CORES = 2
 CHUNK = 8
 PAIRS = 4
-LAG_R = 1
-LAG_F = 2
+LAG_R = 2
+LAG_F = 4
 
 MESH = pl.DeviceIdType.MESH
 F32 = jnp.float32

time: 135 us -> 127 us (0.941)
  Pallas kernels: 131 us -> 124 us
    pallas_call x1, Pallas kernels: 131 us -> 124 us  [local(): pl.pallas_call(functools.partial(kernel, n), out_shape=jax.ShapeDtypeStru...]
where the time goes in v2:
time: 127 us; the launch traced here: 126 us
  Pallas kernels  124 us (98%)
  local copies, waits for them, and re-layouts  2.26 us (2%)
    pallas_call x1, Pallas kernels, local(): pl.pallas_call(functools.partial(kernel, n), out_shape=jax.ShapeDtypeStru...  124 us

profile of v2, /device:TPU:112, one launch (start us, length us, event | category | flops | bytes accessed | tf_op | source)
XLA Modules:
  0.0 126.3 jit_solution(18325922787667020713)
XLA Ops:
  0.0 124.1 %mla_decode.1 = bf16[64,16,512]{2,1,0:T(8,128)(2,1)} custom-call(s32[64]{0:T(128)} %len_ref.1, bf16[64,16,576]{2,1,0:T(8,128)(2,1)} %q_ref.1, bf16[64,576,1024]{2,1,0:T(8,128)(2,1)} %bitcast.ct_ref), custom_call_target="tpu_custom_call" | custom-call | tf_op jit(solution)/shard_map/mla_decode/pallas_call | solution.py:290
  124.1 2.3 %copy.5 = bf16[64,16,512]{2,1,0:T(8,128)(2,1)} copy(bf16[64,16,512]{2,1,0:T(8,128)(2,1)} %mla_decode.1) | data formatting | bytes 2097152

commit v3 on v2

--- a/solution.py
+++ b/solution.py
@@ -28,6 +28,26 @@
     total = functools.reduce(jnp.add, w)
     inv = 1.0 / jnp.maximum(total, 1.0)
     return [x * inv for x in w], top + jnp.log(total)
+
+
+def by_owner(stat, n, hl):
+    t = stat.T[:n]
+    block = lax.broadcasted_iota(jnp.int32, t.shape, 1) // hl
+    row = lax.broadcasted_iota(jnp.int32, t.shape, 0)
+    out = t
+    for r in range(1, n):
+        moved = pltpu.roll(pltpu.roll(t, r * hl, 1), n - r, 0)
+        out = jnp.where((block - row + n) % n == r, moved, out)
+    return out
+
+
+def columns(row):
+    return jnp.broadcast_to(row, (128, 128)).T
+
+
+def scaled(w, i, o):
+    hl, lat = o.shape
+    return jnp.concatenate([w[i * hl:(i + 1) * hl]] * (lat // 128), axis=1) * o.astype(F32)
 
 
 def kernel(n, len_ref, q_ref, ct_ref, o_ref, qraw, qg, od, st, inc, ins, lg, rs, rss, obuf, cbuf,
@@ -164,7 +184,9 @@
             return stat
 
         stat = lax.fori_loop(0, half, pair_step, jnp.full((heads, 128), -jnp.inf, F32))
-        st[:, c, :, :] = stat.reshape(n, hl, 128)
+        lse = by_owner(stat, n, hl)
+        for j in range(n):
+            st[j, c] = lse[j:j + 1]
 
     def rows(c):
         return pl.ds(c * CHUNK, CHUNK)
@@ -212,11 +234,12 @@
             o_wait(c, slot)
         mine = dev(sign(c), k)
         w, lse = weights([st[mine, c], ins[PASS, c], ins[VIA, c], ins[VIA + 1, c]])
+        w = [columns(r) for r in w]
         for i in range(CHUNK):
             b = c * CHUNK + i
-            acc = w[0][:, i:i + 1] * od[mine, b].astype(F32)
+            acc = scaled(w[0], i, od[mine, b])
             for j, slot in ((1, PASS), (2, VIA), (3, VIA + 1)):
-                acc = acc + w[j][:, i:i + 1] * inc[slot, b].astype(F32)
+                acc = acc + scaled(w[j], i, inc[slot, b])
             rs[b] = acc
         rss[c] = lse
         for cp in sum_copies(c):
@@ -231,12 +254,13 @@
         for cp in sum_copies(c):
             cp.wait_recv()
         w, _ = weights([st[me, c], ins[MINE, c], ins[DIRECT, c], ins[DIRECT + 1, c], ins[SUM, c]])
+        w = [columns(r) for r in w]
         for i in range(CHUNK):
             b = c * CHUNK + i
-            acc = w[0][:, i:i + 1] * od[me, b].astype(F32)
+            acc = scaled(w[0], i, od[me, b])
             for j, slot in ((1, MINE), (2, DIRECT), (3, DIRECT + 1)):
-                acc = acc + w[j][:, i:i + 1] * inc[slot, b].astype(F32)
-            acc = acc + w[4][:, i:i + 1] * lg[b]
+                acc = acc + scaled(w[j], i, inc[slot, b])
+            acc = acc + scaled(w[4], i, lg[b])
             obuf[b] = acc.astype(BF16)
         out_copy(c).start()
 
@@ -296,12 +320,12 @@
                 pltpu.VMEM((nb, hl, wd), BF16),
                 pltpu.VMEM((n, nb // 2, hl, 2 * wd), BF16),
                 pltpu.VMEM((n, nb, hl, lat), BF16),
-                pltpu.VMEM((n, nc, hl, 128), F32),
+                pltpu.VMEM((n, nc, 1, 128), F32),
                 pltpu.VMEM((6, nb, hl, lat), BF16),
-                pltpu.VMEM((7, nc, hl, 128), F32),
+                pltpu.VMEM((7, nc, 1, 128), F32),
                 pltpu.VMEM((nb, hl, lat), F32),
                 pltpu.VMEM((nb, hl, lat), F32),
-                pltpu.VMEM((nc, hl, 128), F32),
+                pltpu.VMEM((nc, 1, 128), F32),
                 pltpu.VMEM((nb, hl, lat), BF16),
                 pltpu.VMEM((2 * PAIRS, wd + ROPE, sl), BF16),
                 dma,

time: 127 us -> 126 us (level)
  Pallas kernels: 124 us -> 122 us
    pallas_call x1, Pallas kernels: 124 us -> 122 us  [local(): pl.pallas_call(functools.partial(kernel, n), out_shape=jax.ShapeDtypeStru...]
where the time goes in v3:
time: 126 us; the launch traced here: 125 us
  Pallas kernels  122 us (97%)
  local copies, waits for them, and re-layouts  2.26 us (2%)
    pallas_call x1, Pallas kernels, local(): pl.pallas_call(functools.partial(kernel, n), out_shape=jax.ShapeDtypeStru...  122 us

profile of v3, /device:TPU:112, one launch (start us, length us, event | category | flops | bytes accessed | tf_op | source)
XLA Modules:
  0.0 124.7 jit_solution(16727120594073014922)
XLA Ops:
  0.0 122.4 %mla_decode.1 = bf16[64,16,512]{2,1,0:T(8,128)(2,1)} custom-call(s32[64]{0:T(128)} %len_ref.1, bf16[64,16,576]{2,1,0:T(8,128)(2,1)} %q_ref.1, bf16[64,576,1024]{2,1,0:T(8,128)(2,1)} %bitcast.ct_ref), custom_call_target="tpu_custom_call" | custom-call | tf_op jit(solution)/shard_map/mla_decode/pallas_call | solution.py:314
  122.4 2.3 %copy.5 = bf16[64,16,512]{2,1,0:T(8,128)(2,1)} copy(bf16[64,16,512]{2,1,0:T(8,128)(2,1)} %mla_decode.1) | data formatting | bytes 2097152

commit v4 on v3

--- a/solution.py
+++ b/solution.py
@@ -12,6 +12,8 @@
 CORES = 2
 CHUNK = 8
 PAIRS = 4
+AHEAD = 4
+LEAD = 3
 LAG_R = 2
 LAG_F = 4
 
@@ -128,7 +130,7 @@
         q_copy(2, me, c, partner).start()
         return 0
 
-    lax.fori_loop(0, nc, q0, 0)
+    lax.fori_loop(0, AHEAD, q0, 0)
 
     def q1(c, _):
         way = -sign(c)
@@ -137,9 +139,14 @@
         q_wait(1, dev(1, k), c)
         q_copy(4, dev(1, k), c, partner).start()
         q_copy(5, dev(-way, k), c, dev(way, k)).start()
-        return 0
-
-    lax.fori_loop(0, nc, q1, 0)
+
+        @pl.when(c + AHEAD < nc)
+        def _():
+            q0(c + AHEAD, 0)
+
+        return 0
+
+    lax.fori_loop(0, LEAD, q1, 0)
 
     def q2(c):
         q_wait(5, dev(2, k), c)
@@ -264,11 +271,17 @@
             obuf[b] = acc.astype(BF16)
         out_copy(c).start()
 
-    q2(0)
-
     def step(t, _):
+        @pl.when(t + LEAD < nc)
+        def _():
+            q1(t + LEAD, 0)
+
         @pl.when(t < nc)
         def _():
+            @pl.when(t == 0)
+            def _():
+                q2(0)
+
             @pl.when(t + 1 < nc)
             def _():
                 q2(t + 1)

time: 126 us -> 122 us (0.968)
  Pallas kernels: 122 us -> 119 us
    pallas_call x1, Pallas kernels: 122 us -> 119 us  [local(): pl.pallas_call(functools.partial(kernel, n), out_shape=jax.ShapeDtypeStru...]
where the time goes in v4:
time: 122 us; the launch traced here: 121 us
  Pallas kernels  119 us (98%)
  local copies, waits for them, and re-layouts  2.26 us (2%)
    pallas_call x1, Pallas kernels, local(): pl.pallas_call(functools.partial(kernel, n), out_shape=jax.ShapeDtypeStru...  119 us

profile of v4, /device:TPU:112, one launch (start us, length us, event | category | flops | bytes accessed | tf_op | source)
XLA Modules:
  0.0 121.4 jit_solution(17283760762908268643)
XLA Ops:
  0.0 119.2 %mla_decode.1 = bf16[64,16,512]{2,1,0:T(8,128)(2,1)} custom-call(s32[64]{0:T(128)} %len_ref.1, bf16[64,16,576]{2,1,0:T(8,128)(2,1)} %q_ref.1, bf16[64,576,1024]{2,1,0:T(8,128)(2,1)} %bitcast.ct_ref), custom_call_target="tpu_custom_call" | custom-call | tf_op jit(solution)/shard_map/mla_decode/pallas_call | solution.py:327
  119.2 2.3 %copy.5 = bf16[64,16,512]{2,1,0:T(8,128)(2,1)} copy(bf16[64,16,512]{2,1,0:T(8,128)(2,1)} %mla_decode.1) | data formatting | bytes 2097152

commit v5 on v4

--- a/solution.py
+++ b/solution.py
@@ -52,8 +52,8 @@
     return jnp.concatenate([w[i * hl:(i + 1) * hl]] * (lat // 128), axis=1) * o.astype(F32)
 
 
-def kernel(n, len_ref, q_ref, ct_ref, o_ref, qraw, qg, od, st, inc, ins, lg, rs, rss, obuf, cbuf,
-           raw_sem, cache_sem, out_sem, q_send, q_recv, o_send, o_recv, t_send, t_recv):
+def kernel(n, len_ref, q_ref, ct_ref, o_ref, qraw, qg, od, st, inc, ins, lg, rs, rss, cbuf,
+           raw_sem, cache_sem, q_send, q_recv, o_send, o_recv, t_send, t_recv):
     chips = n // CORES
     nb, hl, wd = q_ref.shape
     lat = wd - ROPE
@@ -94,9 +94,6 @@
     for peer in peers:
         pl.semaphore_signal(barrier, inc=1, device_id={'dcp': peer}, device_id_type=MESH)
 
-    for g in range(PAIRS):
-        cbuf[2 * g, pl.ds(wd, ROPE), :] = jnp.zeros((ROPE, sl), BF16)
-        cbuf[2 * g + 1, pl.ds(lat, ROPE), :] = jnp.zeros((ROPE, sl), BF16)
     raw.wait()
 
     def pack(g, _):
@@ -107,9 +104,7 @@
         qg[me, g, :, pl.ds(2 * lat, 2 * ROPE)] = jnp.concatenate([r0, r1], axis=1)
         return 0
 
-    lax.fori_loop(0, npair, pack, 0)
-    for g in range(PAIRS):
-        fetch(g)
+    lax.fori_loop(0, half, pack, 0)
     pl.semaphore_wait(barrier, len(peers))
 
     def q_copy(kind, src, c, to):
@@ -125,12 +120,21 @@
         return 1 - 2 * (c % 2)
 
     def q0(c, _):
+        @pl.when(c + 1 < nc)
+        def _():
+            lax.fori_loop((c + 1) * half, (c + 2) * half, pack, 0)
+
         q_copy(0, me, c, dev(1, k)).start()
         q_copy(1, me, c, dev(-1, k)).start()
         q_copy(2, me, c, partner).start()
         return 0
 
     lax.fori_loop(0, AHEAD, q0, 0)
+
+    for g in range(PAIRS):
+        fetch(g)
+        cbuf[2 * g, pl.ds(wd, ROPE), :] = jnp.zeros((ROPE, sl), BF16)
+        cbuf[2 * g + 1, pl.ds(lat, ROPE), :] = jnp.zeros((ROPE, sl), BF16)
 
     def q1(c, _):
         way = -sign(c)
@@ -252,9 +256,6 @@
         for cp in sum_copies(c):
             cp.start()
 
-    def out_copy(c):
-        return pltpu.make_async_copy(obuf.at[rows(c)], o_ref.at[rows(c)], out_sem.at[c])
-
     def merge(c):
         for slot in (MINE, DIRECT, DIRECT + 1):
             o_wait(c, slot)
@@ -268,8 +269,7 @@
             for j, slot in ((1, MINE), (2, DIRECT), (3, DIRECT + 1)):
                 acc = acc + scaled(w[j], i, inc[slot, b])
             acc = acc + scaled(w[4], i, lg[b])
-            obuf[b] = acc.astype(BF16)
-        out_copy(c).start()
+            o_ref[b] = acc.astype(BF16)
 
     def step(t, _):
         @pl.when(t + LEAD < nc)
@@ -308,7 +308,6 @@
             q_copy(kind, me, c, me).wait_send()
         for cp in sends(c) + sum_copies(c):
             cp.wait_send()
-        out_copy(c).wait()
         return 0
 
     lax.fori_loop(0, nc, drain, 0)
@@ -326,9 +325,9 @@
         dma = pltpu.SemaphoreType.DMA
         return pl.pallas_call(
             functools.partial(kernel, n),
-            out_shape=jax.ShapeDtypeStruct((nb, hl, lat), BF16),
+            out_shape=pltpu.VMEM((nb, hl, lat), BF16),
             in_specs=[pl.BlockSpec(memory_space=pltpu.SMEM), anyspace, anyspace],
-            out_specs=anyspace,
+            out_specs=pl.BlockSpec(memory_space=pltpu.VMEM),
             scratch_shapes=[
                 pltpu.VMEM((nb, hl, wd), BF16),
                 pltpu.VMEM((n, nb // 2, hl, 2 * wd), BF16),
@@ -339,11 +338,9 @@
                 pltpu.VMEM((nb, hl, lat), F32),
                 pltpu.VMEM((nb, hl, lat), F32),
                 pltpu.VMEM((nc, 1, 128), F32),
-                pltpu.VMEM((nb, hl, lat), BF16),
                 pltpu.VMEM((2 * PAIRS, wd + ROPE, sl), BF16),
                 dma,
                 dma((2 * PAIRS, 2)),
-                dma((nc,)),
                 dma((7, nc)),
                 dma((7, nc)),
                 dma((7, nc)),
@@ -352,7 +349,7 @@
                 dma((7, nc)),
             ],
             compiler_params=pltpu.CompilerParams(
-                collective_id=0, has_side_effects=True, vmem_limit_bytes=63 * 1024 * 1024),
+                collective_id=0, has_side_effects=True, vmem_limit_bytes=56 * 1024 * 1024),
             name='mla_decode',
         )(lengths, q, jnp.swapaxes(cache, 1, 2))
 

time: 122 us -> 118 us (0.967)
  Pallas kernels: 119 us -> 117 us
  local copies, waits for them, and re-layouts: 2.26 us -> 0.97 us
    pallas_call x1, Pallas kernels: 119 us -> 117 us  [local(): pl.pallas_call(functools.partial(kernel, n), out_shape=pltpu.VMEM((nb, hl...]
    unnamed x1, local copies, waits for them, and re-layouts: 2.26 us -> 0.97 us
where the time goes in v5:
time: 118 us
  Pallas kernels  117 us (99%)
    pallas_call x1, Pallas kernels, local(): pl.pallas_call(functools.partial(kernel, n), out_shape=pltpu.VMEM((nb, hl...  117 us

profile of v5, /device:TPU:112, one launch (start us, length us, event | category | flops | bytes accessed | tf_op | source)
XLA Modules:
  0.0 118.0 jit_solution(8678565924360335217)
XLA Ops:
  0.0 117.0 %mla_decode.1 = bf16[64,16,512]{2,1,0:T(8,128)(2,1)S(1)} custom-call(s32[64]{0:T(128)} %len_ref.1, bf16[64,16,576]{2,1,0:T(8,128)(2,1)} %q_ref.1, bf16[64,576,1024]{2,1,0:T(8,128)(2,1)} %bitcast.ct_ref), custom_call_target="tpu_custom_call" | custom-call | tf_op jit(solution)/shard_map/mla_decode/pallas_call | solution.py:326
  117.0 1.0 copy.5

commit v6 on v5

--- a/solution.py
+++ b/solution.py
@@ -10,12 +10,12 @@
 ROPE = 64
 SCALE = 192 ** -0.5
 CORES = 2
-CHUNK = 8
+CHUNK = 4
 PAIRS = 4
-AHEAD = 4
-LEAD = 3
-LAG_R = 2
-LAG_F = 4
+AHEAD = 8
+LEAD = 6
+LAG_R = 4
+LAG_F = 8
 
 MESH = pl.DeviceIdType.MESH
 F32 = jnp.float32

time: 118 us -> 122 us (1.034)
  Pallas kernels: 117 us -> 120 us
    pallas_call x1, Pallas kernels: 117 us -> 120 us  [local(): pl.pallas_call(functools.partial(kernel, n), out_shape=pltpu.VMEM((nb, hl...]
where the time goes in v6:
time: 122 us; the launch traced here: 121 us
  Pallas kernels  120 us (98%)
    pallas_call x1, Pallas kernels, local(): pl.pallas_call(functools.partial(kernel, n), out_shape=pltpu.VMEM((nb, hl...  120 us

profile of v6, /device:TPU:112, one launch (start us, length us, event | category | flops | bytes accessed | tf_op | source)
XLA Modules:
  0.0 121.5 jit_solution(18211697690677120839)
XLA Ops:
  0.0 120.5 %mla_decode.1 = bf16[64,16,512]{2,1,0:T(8,128)(2,1)S(1)} custom-call(s32[64]{0:T(128)} %len_ref.1, bf16[64,16,576]{2,1,0:T(8,128)(2,1)} %q_ref.1, bf16[64,576,1024]{2,1,0:T(8,128)(2,1)} %bitcast.ct_ref), custom_call_target="tpu_custom_call" | custom-call | tf_op jit(solution)/shard_map/mla_decode/pallas_call | solution.py:326
  120.5 1.0 copy.5

commit v7 on v5

--- a/solution.py
+++ b/solution.py
@@ -14,13 +14,15 @@
 PAIRS = 4
 AHEAD = 4
 LEAD = 3
-LAG_R = 2
-LAG_F = 4
+LAG_V = 2
+LAG_R = 3
+LAG_D = 4
+LAG_F = 6
 
 MESH = pl.DeviceIdType.MESH
 F32 = jnp.float32
 BF16 = jnp.bfloat16
-VIA, DIRECT, MINE, PASS, SUM = 0, 2, 4, 5, 6
+VIA, DIRECT, MINE, PASS, VIA2, DIRECT2, SUM = range(7)
 
 
 def weights(stats):
@@ -52,7 +54,7 @@
     return jnp.concatenate([w[i * hl:(i + 1) * hl]] * (lat // 128), axis=1) * o.astype(F32)
 
 
-def kernel(n, len_ref, q_ref, ct_ref, o_ref, qraw, qg, od, st, inc, ins, lg, rs, rss, cbuf,
+def kernel(n, len_ref, q_ref, ct_ref, o_ref, qraw, qg, od, st, two, twos, inc, ins, lg, rs, rss, cbuf,
            raw_sem, cache_sem, q_send, q_recv, o_send, o_recv, t_send, t_recv):
     chips = n // CORES
     nb, hl, wd = q_ref.shape
@@ -185,7 +187,7 @@
                 pv = lax.dot_general(p.astype(BF16), cbuf[slot, pl.ds(0, lat), :], (((1,), (1,)), ((), ())),
                                      preferred_element_type=F32)
                 o = (pv * (1.0 / jnp.maximum(l, 1.0))).astype(BF16)
-                od[:, b, :, :] = o.reshape(n, hl, lat)
+                od[:, b] = o.reshape(chips, CORES, hl, lat)
                 stat = jnp.where(lane == i * 2 + par, m + jnp.log(l), stat)
 
             @pl.when(g + PAIRS < npair)
@@ -197,77 +199,85 @@
         stat = lax.fori_loop(0, half, pair_step, jnp.full((heads, 128), -jnp.inf, F32))
         lse = by_owner(stat, n, hl)
         for j in range(n):
-            st[j, c] = lse[j:j + 1]
+            st[j // CORES, c, j % CORES] = lse[j:j + 1]
 
     def rows(c):
         return pl.ds(c * CHUNK, CHUNK)
 
-    def o_copies(c, head, slot_s, slot_r, to):
+    def o_copies(c, kind, src, srcs, dst, dsts, to):
         return [
             pltpu.make_async_remote_copy(
-                src_ref=od.at[head, rows(c)], dst_ref=inc.at[slot_r, rows(c)],
-                send_sem=o_send.at[slot_s, c], recv_sem=o_recv.at[slot_r, c],
+                src_ref=src, dst_ref=dst, send_sem=o_send.at[kind, c], recv_sem=o_recv.at[kind, c],
                 device_id={'dcp': to}, device_id_type=MESH),
             pltpu.make_async_remote_copy(
-                src_ref=st.at[head, c], dst_ref=ins.at[slot_r, c],
-                send_sem=t_send.at[slot_s, c], recv_sem=t_recv.at[slot_r, c],
+                src_ref=srcs, dst_ref=dsts, send_sem=t_send.at[kind, c], recv_sem=t_recv.at[kind, c],
                 device_id={'dcp': to}, device_id_type=MESH),
         ]
 
+    def to_chip(c, kind, head, step):
+        return o_copies(c, kind, od.at[head, rows(c)], st.at[head, c], two.at[kind, rows(c)], twos.at[kind, c],
+                        dev(step, k))
+
+    def to_partner(c, kind, src, srcs):
+        return o_copies(c, kind, src, srcs, inc.at[kind - MINE, rows(c)], ins.at[kind, c], partner)
+
+    def chip(step):
+        return (x + step + chips) % chips
+
     def sends(c):
         way = sign(c)
-        out = []
-        for kk in range(CORES):
-            out += o_copies(c, dev(2, kk), VIA + kk, VIA + k, dev(way, kk))
-        out += o_copies(c, dev(way, 1 - k), PASS, PASS, partner)
-        out += o_copies(c, partner, MINE, MINE, partner)
-        for kk in range(CORES):
-            out += o_copies(c, dev(-way, kk), DIRECT + kk, DIRECT + k, dev(-way, kk))
-        return out
+        relayed = chip(way)
+        return (to_chip(c, VIA, chip(2), way)
+                + to_partner(c, PASS, od.at[relayed, rows(c), 1 - k], st.at[relayed, c, 1 - k])
+                + to_partner(c, MINE, od.at[x, rows(c), 1 - k], st.at[x, c, 1 - k])
+                + to_chip(c, DIRECT, chip(-way), -way))
+
+    def share(c, kind):
+        return to_partner(c, kind + VIA2, two.at[kind, rows(c), 1 - k], twos.at[kind, c, 1 - k])
+
+    def pass_on(c, kind):
+        for cp in to_chip(c, kind, x, 0):
+            cp.wait_recv()
+        for cp in share(c, kind):
+            cp.start()
+
+    def partner_wait(c, kind):
+        for cp in to_partner(c, kind, inc.at[kind - MINE, rows(c)], ins.at[kind, c]):
+            cp.wait_recv()
 
     def sum_copies(c):
-        to = dev(sign(c), k)
-        return [
-            pltpu.make_async_remote_copy(
-                src_ref=rs.at[rows(c)], dst_ref=lg.at[rows(c)], send_sem=o_send.at[SUM, c], recv_sem=o_recv.at[SUM, c],
-                device_id={'dcp': to}, device_id_type=MESH),
-            pltpu.make_async_remote_copy(
-                src_ref=rss.at[c], dst_ref=ins.at[SUM, c], send_sem=t_send.at[SUM, c], recv_sem=t_recv.at[SUM, c],
-                device_id={'dcp': to}, device_id_type=MESH),
-        ]
-
-    def o_wait(c, slot):
-        for cp in o_copies(c, me, slot, slot, me):
-            cp.wait_recv()
+        return o_copies(c, SUM, rs.at[rows(c)], rss.at[c], lg.at[rows(c)], ins.at[SUM, c], dev(sign(c), k))
 
     def relay(c):
-        for slot in (PASS, VIA, VIA + 1):
-            o_wait(c, slot)
-        mine = dev(sign(c), k)
-        w, lse = weights([st[mine, c], ins[PASS, c], ins[VIA, c], ins[VIA + 1, c]])
+        for kind in (PASS, VIA2):
+            partner_wait(c, kind)
+        mine = chip(sign(c))
+        w, lse = weights([st[mine, c, k], ins[PASS, c], twos[VIA, c, k], ins[VIA2, c]])
         w = [columns(r) for r in w]
         for i in range(CHUNK):
             b = c * CHUNK + i
-            acc = scaled(w[0], i, od[mine, b])
-            for j, slot in ((1, PASS), (2, VIA), (3, VIA + 1)):
-                acc = acc + scaled(w[j], i, inc[slot, b])
+            acc = scaled(w[0], i, od[mine, b, k])
+            acc = acc + scaled(w[1], i, inc[PASS - MINE, b])
+            acc = acc + scaled(w[2], i, two[VIA, b, k])
+            acc = acc + scaled(w[3], i, inc[VIA2 - MINE, b])
             rs[b] = acc
         rss[c] = lse
         for cp in sum_copies(c):
             cp.start()
 
     def merge(c):
-        for slot in (MINE, DIRECT, DIRECT + 1):
-            o_wait(c, slot)
+        for kind in (MINE, DIRECT2):
+            partner_wait(c, kind)
         for cp in sum_copies(c):
             cp.wait_recv()
-        w, _ = weights([st[me, c], ins[MINE, c], ins[DIRECT, c], ins[DIRECT + 1, c], ins[SUM, c]])
+        w, _ = weights([st[x, c, k], ins[MINE, c], twos[DIRECT, c, k], ins[DIRECT2, c], ins[SUM, c]])
         w = [columns(r) for r in w]
         for i in range(CHUNK):
             b = c * CHUNK + i
-            acc = scaled(w[0], i, od[me, b])
-            for j, slot in ((1, MINE), (2, DIRECT), (3, DIRECT + 1)):
-                acc = acc + scaled(w[j], i, inc[slot, b])
+            acc = scaled(w[0], i, od[x, b, k])
+            acc = acc + scaled(w[1], i, inc[MINE - MINE, b])
+            acc = acc + scaled(w[2], i, two[DIRECT, b, k])
+            acc = acc + scaled(w[3], i, inc[DIRECT2 - MINE, b])
             acc = acc + scaled(w[4], i, lg[b])
             o_ref[b] = acc.astype(BF16)
 
@@ -291,9 +301,17 @@
             for cp in sends(t):
                 cp.start()
 
+        @pl.when(jnp.logical_and(t >= LAG_V, t < nc + LAG_V))
+        def _():
+            pass_on(t - LAG_V, VIA)
+
         @pl.when(jnp.logical_and(t >= LAG_R, t < nc + LAG_R))
         def _():
             relay(t - LAG_R)
+
+        @pl.when(jnp.logical_and(t >= LAG_D, t < nc + LAG_D))
+        def _():
+            pass_on(t - LAG_D, DIRECT)
 
         @pl.when(t >= LAG_F)
         def _():
@@ -306,7 +324,7 @@
     def drain(c, _):
         for kind in range(7):
             q_copy(kind, me, c, me).wait_send()
-        for cp in sends(c) + sum_copies(c):
+        for cp in sends(c) + share(c, VIA) + share(c, DIRECT) + sum_copies(c):
             cp.wait_send()
         return 0
 
@@ -331,9 +349,11 @@
             scratch_shapes=[
                 pltpu.VMEM((nb, hl, wd), BF16),
                 pltpu.VMEM((n, nb // 2, hl, 2 * wd), BF16),
-                pltpu.VMEM((n, nb, hl, lat), BF16),
-                pltpu.VMEM((n, nc, 1, 128), F32),
-                pltpu.VMEM((6, nb, hl, lat), BF16),
+                pltpu.VMEM((n // CORES, nb, CORES, hl, lat), BF16),
+                pltpu.VMEM((n // CORES, nc, CORES, 1, 128), F32),
+                pltpu.VMEM((2, nb, CORES, hl, lat), BF16),
+                pltpu.VMEM((2, nc, CORES, 1, 128), F32),
+                pltpu.VMEM((4, nb, hl, lat), BF16),
                 pltpu.VMEM((7, nc, 1, 128), F32),
                 pltpu.VMEM((nb, hl, lat), F32),
                 pltpu.VMEM((nb, hl, lat), F32),

time: 118 us -> 118 us (level)
  no operation moved by 1% of the time
where the time goes in v7:
time: 118 us
  Pallas kernels  117 us (99%)
    pallas_call x1, Pallas kernels, local(): pl.pallas_call(functools.partial(kernel, n), out_shape=pltpu.VMEM((nb, hl...  117 us

profile of v7, /device:TPU:112, one launch (start us, length us, event | category | flops | bytes accessed | tf_op | source)
XLA Modules:
  0.0 117.8 jit_solution(8079103859645473263)
XLA Ops:
  0.0 116.8 %mla_decode.1 = bf16[64,16,512]{2,1,0:T(8,128)(2,1)S(1)} custom-call(s32[64]{0:T(128)} %len_ref.1, bf16[64,16,576]{2,1,0:T(8,128)(2,1)} %q_ref.1, bf16[64,576,1024]{2,1,0:T(8,128)(2,1)} %bitcast.ct_ref), custom_call_target="tpu_custom_call" | custom-call | tf_op jit(solution)/shard_map/mla_decode/pallas_call | solution.py:344
  116.8 1.0 copy.5

commit v8 on v7

--- a/solution.py
+++ b/solution.py
@@ -168,35 +168,51 @@
     where_t = lax.broadcasted_iota(jnp.int32, (1, sl), 1)
     base = me * sl
 
+    def arrive(g):
+        for par in range(2):
+            for cp in cache_copies(g, par):
+                cp.wait()
+
+    def scores(g, par):
+        b = g * 2 + par
+        slot = (g % PAIRS) * 2 + par
+        qa = qg[:, g, :, pl.ds(par * lat, lat)].reshape(heads, lat)
+        qr = qg[:, g, :, pl.ds(2 * lat, 2 * ROPE)].reshape(heads, 2 * ROPE)
+        s = jnp.dot(qa, cbuf[slot, pl.ds(0, lat), :], preferred_element_type=F32)
+        s = s + jnp.dot(qr, cbuf[slot, pl.ds(lat, 2 * ROPE), :], preferred_element_type=F32)
+        return jnp.where(where_t < len_ref[b] - base, s * SCALE, -jnp.inf)
+
+    def finish(g, par, s):
+        b = g * 2 + par
+        slot = (g % PAIRS) * 2 + par
+        m = jnp.maximum(jnp.max(s, axis=1, keepdims=True), jnp.finfo(F32).min)
+        p = jnp.exp(s - m)
+        l = jnp.sum(p, axis=1, keepdims=True)
+        pv = lax.dot_general(p.astype(BF16), cbuf[slot, pl.ds(0, lat), :], (((1,), (1,)), ((), ())),
+                             preferred_element_type=F32)
+        o = (pv * (1.0 / jnp.maximum(l, 1.0))).astype(BF16)
+        od[:, b] = o.reshape(chips, CORES, hl, lat)
+        return m + jnp.log(l)
+
     def attend(c):
-        def pair_step(i, stat):
-            g = c * half + i
-            for par in range(2):
-                b = g * 2 + par
-                slot = (g % PAIRS) * 2 + par
-                for cp in cache_copies(g, par):
-                    cp.wait()
-                qa = qg[:, g, :, pl.ds(par * lat, lat)].reshape(heads, lat)
-                qr = qg[:, g, :, pl.ds(2 * lat, 2 * ROPE)].reshape(heads, 2 * ROPE)
-                s = jnp.dot(qa, cbuf[slot, pl.ds(0, lat), :], preferred_element_type=F32)
-                s = s + jnp.dot(qr, cbuf[slot, pl.ds(lat, 2 * ROPE), :], preferred_element_type=F32)
-                s = jnp.where(where_t < len_ref[b] - base, s * SCALE, -jnp.inf)
-                m = jnp.maximum(jnp.max(s, axis=1, keepdims=True), jnp.finfo(F32).min)
-                p = jnp.exp(s - m)
-                l = jnp.sum(p, axis=1, keepdims=True)
-                pv = lax.dot_general(p.astype(BF16), cbuf[slot, pl.ds(0, lat), :], (((1,), (1,)), ((), ())),
-                                     preferred_element_type=F32)
-                o = (pv * (1.0 / jnp.maximum(l, 1.0))).astype(BF16)
-                od[:, b] = o.reshape(chips, CORES, hl, lat)
-                stat = jnp.where(lane == i * 2 + par, m + jnp.log(l), stat)
+        stat = jnp.full((heads, 128), -jnp.inf, F32)
+        first = c * half
+        arrive(first)
+        s0 = scores(first, 0)
+        for i in range(half):
+            g = first + i
+            if i + 1 < half:
+                arrive(g + 1)
+            s1 = scores(g, 1)
+            stat = jnp.where(lane == 2 * i, finish(g, 0, s0), stat)
+            if i + 1 < half:
+                s0 = scores(g + 1, 0)
+            stat = jnp.where(lane == 2 * i + 1, finish(g, 1, s1), stat)
 
             @pl.when(g + PAIRS < npair)
             def _():
                 fetch(g + PAIRS)
 
-            return stat
-
-        stat = lax.fori_loop(0, half, pair_step, jnp.full((heads, 128), -jnp.inf, F32))
         lse = by_owner(stat, n, hl)
         for j in range(n):
             st[j // CORES, c, j % CORES] = lse[j:j + 1]

time: 118 us -> 118 us (level)
  no operation moved by 1% of the time
where the time goes in v8:
time: 118 us
  Pallas kernels  117 us (99%)
    pallas_call x1, Pallas kernels, local(): pl.pallas_call(functools.partial(kernel, n), out_shape=pltpu.VMEM((nb, hl...  117 us

profile of v8, /device:TPU:112, one launch (start us, length us, event | category | flops | bytes accessed | tf_op | source)
XLA Modules:
  0.0 117.8 jit_solution(11684877413455494032)
XLA Ops:
  0.0 116.8 %mla_decode.1 = bf16[64,16,512]{2,1,0:T(8,128)(2,1)S(1)} custom-call(s32[64]{0:T(128)} %len_ref.1, bf16[64,16,576]{2,1,0:T(8,128)(2,1)} %q_ref.1, bf16[64,576,1024]{2,1,0:T(8,128)(2,1)} %bitcast.ct_ref), custom_call_target="tpu_custom_call" | custom-call | tf_op jit(solution)/shard_map/mla_decode/pallas_call | solution.py:360
  116.8 1.0 copy.5

commit v9 on v8

--- a/solution.py
+++ b/solution.py
@@ -54,8 +54,8 @@
     return jnp.concatenate([w[i * hl:(i + 1) * hl]] * (lat // 128), axis=1) * o.astype(F32)
 
 
-def kernel(n, len_ref, q_ref, ct_ref, o_ref, qraw, qg, od, st, two, twos, inc, ins, lg, rs, rss, cbuf,
-           raw_sem, cache_sem, q_send, q_recv, o_send, o_recv, t_send, t_recv):
+def kernel(n, len_hbm, q_ref, ct_ref, o_ref, len_ref, qraw, qg, od, st, two, twos, inc, ins, lg, rs, rss, cbuf,
+           len_sem, raw_sem, cache_sem, q_send, q_recv, o_send, o_recv, t_send, t_recv):
     chips = n // CORES
     nb, hl, wd = q_ref.shape
     lat = wd - ROPE
@@ -88,15 +88,19 @@
             for cp in cache_copies(pair, par):
                 cp.start()
 
-    raw = pltpu.make_async_copy(q_ref, qraw, raw_sem)
-    raw.start()
-
     barrier = pltpu.get_barrier_semaphore()
-    peers = [partner, dev(1, 0), dev(1, 1), dev(-1, 0), dev(-1, 1)]
+    peers = [dev(1, k), dev(-1, k), partner]
     for peer in peers:
         pl.semaphore_signal(barrier, inc=1, device_id={'dcp': peer}, device_id_type=MESH)
 
-    raw.wait()
+    def raw(c):
+        part = pl.ds(c * CHUNK, CHUNK)
+        return pltpu.make_async_copy(q_ref.at[part], qraw.at[part], raw_sem.at[c])
+
+    for c in range(nc):
+        raw(c).start()
+    lengths = pltpu.make_async_copy(len_hbm, len_ref, len_sem)
+    lengths.start()
 
     def pack(g, _):
         for par in range(2):
@@ -106,6 +110,7 @@
         qg[me, g, :, pl.ds(2 * lat, 2 * ROPE)] = jnp.concatenate([r0, r1], axis=1)
         return 0
 
+    raw(0).wait()
     lax.fori_loop(0, half, pack, 0)
     pl.semaphore_wait(barrier, len(peers))
 
@@ -124,6 +129,7 @@
     def q0(c, _):
         @pl.when(c + 1 < nc)
         def _():
+            raw(c + 1).wait()
             lax.fori_loop((c + 1) * half, (c + 2) * half, pack, 0)
 
         q_copy(0, me, c, dev(1, k)).start()
@@ -153,6 +159,7 @@
         return 0
 
     lax.fori_loop(0, LEAD, q1, 0)
+    lengths.wait()
 
     def q2(c):
         q_wait(5, dev(2, k), c)
@@ -360,9 +367,10 @@
         return pl.pallas_call(
             functools.partial(kernel, n),
             out_shape=pltpu.VMEM((nb, hl, lat), BF16),
-            in_specs=[pl.BlockSpec(memory_space=pltpu.SMEM), anyspace, anyspace],
+            in_specs=[anyspace, anyspace, anyspace],
             out_specs=pl.BlockSpec(memory_space=pltpu.VMEM),
             scratch_shapes=[
+                pltpu.SMEM((nb,), jnp.int32),
                 pltpu.VMEM((nb, hl, wd), BF16),
                 pltpu.VMEM((n, nb // 2, hl, 2 * wd), BF16),
                 pltpu.VMEM((n // CORES, nb, CORES, hl, lat), BF16),
@@ -376,6 +384,7 @@
                 pltpu.VMEM((nc, 1, 128), F32),
                 pltpu.VMEM((2 * PAIRS, wd + ROPE, sl), BF16),
                 dma,
+                dma((nc,)),
                 dma((2 * PAIRS, 2)),
                 dma((7, nc)),
                 dma((7, nc)),

time: 118 us -> 117 us (level)
  no operation moved by 1% of the time
where the time goes in v9:
time: 117 us
  Pallas kernels  116 us (99%)
    pallas_call x1, Pallas kernels, local(): pl.pallas_call(functools.partial(kernel, n), out_shape=pltpu.VMEM((nb, hl...  116 us

profile of v9, /device:TPU:112, one launch (start us, length us, event | category | flops | bytes accessed | tf_op | source)
XLA Modules:
  0.0 116.8 jit_solution(6540838062548685470)
XLA Ops:
  0.0 115.8 %mla_decode.1 = bf16[64,16,512]{2,1,0:T(8,128)(2,1)S(1)} custom-call(s32[64]{0:T(128)} %len_hbm.1, bf16[64,16,576]{2,1,0:T(8,128)(2,1)} %q_ref.1, bf16[64,576,1024]{2,1,0:T(8,128)(2,1)} %bitcast.ct_ref), custom_call_target="tpu_custom_call" | custom-call | tf_op jit(solution)/shard_map/mla_decode/pallas_call | solution.py:367
  115.8 1.0 copy.5

commit v10 on v9

--- a/solution.py
+++ b/solution.py
@@ -22,6 +22,7 @@
 MESH = pl.DeviceIdType.MESH
 F32 = jnp.float32
 BF16 = jnp.bfloat16
+OWN, PARTNERS, PASSED, OWN2, NEAR2, FAR2 = range(6)
 VIA, DIRECT, MINE, PASS, VIA2, DIRECT2, SUM = range(7)
 
 
@@ -104,27 +105,50 @@
 
     def pack(g, _):
         for par in range(2):
-            qg[me, g, :, pl.ds(par * lat, lat)] = qraw[2 * g + par, :, pl.ds(0, lat)]
+            qg[x, g, k, :, pl.ds(par * lat, lat)] = qraw[2 * g + par, :, pl.ds(0, lat)]
         r0 = qraw[2 * g, :, pl.ds(lat, ROPE)]
         r1 = qraw[2 * g + 1, :, pl.ds(lat, ROPE)]
-        qg[me, g, :, pl.ds(2 * lat, 2 * ROPE)] = jnp.concatenate([r0, r1], axis=1)
+        qg[x, g, k, :, pl.ds(2 * lat, 2 * ROPE)] = jnp.concatenate([r0, r1], axis=1)
         return 0
 
     raw(0).wait()
     lax.fori_loop(0, half, pack, 0)
     pl.semaphore_wait(barrier, len(peers))
 
-    def q_copy(kind, src, c, to):
-        part = qg.at[src, pl.ds(c * half, half)]
+    def sign(c):
+        return 1 - 2 * (c % 2)
+
+    ahead = 2 * k - 1
+
+    def q_copy(kind, chip, core, c, to):
+        part = qg.at[chip, pl.ds(c * half, half)] if core is None else qg.at[chip, pl.ds(c * half, half), core]
         return pltpu.make_async_remote_copy(
             src_ref=part, dst_ref=part, send_sem=q_send.at[kind, c], recv_sem=q_recv.at[kind, c],
             device_id={'dcp': to}, device_id_type=MESH)
 
-    def q_wait(kind, src, c):
-        q_copy(kind, src, c, me).wait_recv()
-
-    def sign(c):
-        return 1 - 2 * (c % 2)
+    def chip(step):
+        return (x + step + chips) % chips
+
+    def relays(c):
+        return c % 2 == k
+
+    def own(c):
+        return q_copy(OWN, x, k, c, dev(ahead, k))
+
+    def own_share(c):
+        return q_copy(OWN2, x, k, c, partner)
+
+    def partners(c):
+        return q_copy(PARTNERS, x, 1 - k, c, dev(ahead, k))
+
+    def near_share(c):
+        return q_copy(NEAR2, chip(-ahead), None, c, partner)
+
+    def passed(c):
+        return q_copy(PASSED, chip(-ahead), None, c, dev(ahead, k))
+
+    def far_share(c):
+        return q_copy(FAR2, chip(2), None, c, partner)
 
     def q0(c, _):
         @pl.when(c + 1 < nc)
@@ -132,12 +156,18 @@
             raw(c + 1).wait()
             lax.fori_loop((c + 1) * half, (c + 2) * half, pack, 0)
 
-        q_copy(0, me, c, dev(1, k)).start()
-        q_copy(1, me, c, dev(-1, k)).start()
-        q_copy(2, me, c, partner).start()
+        own(c).start()
+        own_share(c).start()
         return 0
 
-    lax.fori_loop(0, AHEAD, q0, 0)
+    def q0b(c):
+        q_copy(OWN2, x, 1 - k, c, me).wait_recv()
+        partners(c).start()
+
+    for c in range(AHEAD):
+        q0(c, 0)
+        if c > 0:
+            q0b(c - 1)
 
     for g in range(PAIRS):
         fetch(g)
@@ -145,16 +175,21 @@
         cbuf[2 * g + 1, pl.ds(lat, ROPE), :] = jnp.zeros((ROPE, sl), BF16)
 
     def q1(c, _):
-        way = -sign(c)
-        q_wait(0, dev(-1, k), c)
-        q_copy(3, dev(-1, k), c, partner).start()
-        q_wait(1, dev(1, k), c)
-        q_copy(4, dev(1, k), c, partner).start()
-        q_copy(5, dev(-way, k), c, dev(way, k)).start()
+        q_copy(OWN, chip(-ahead), k, c, me).wait_recv()
+        q_copy(PARTNERS, chip(-ahead), 1 - k, c, me).wait_recv()
+        near_share(c).start()
+
+        @pl.when(relays(c))
+        def _():
+            passed(c).start()
 
         @pl.when(c + AHEAD < nc)
         def _():
             q0(c + AHEAD, 0)
+
+        @pl.when(c + AHEAD - 1 < nc)
+        def _():
+            q0b(c + AHEAD - 1)
 
         return 0
 
@@ -162,14 +197,17 @@
     lengths.wait()
 
     def q2(c):
-        q_wait(5, dev(2, k), c)
-        q_copy(6, dev(2, k), c, partner).start()
+        @pl.when(relays(c))
+        def _():
+            q_copy(PASSED, chip(2), None, c, me).wait_recv()
+            far_share(c).start()
 
     def q3(c):
-        q_wait(2, partner, c)
-        q_wait(3, dev(-1, 1 - k), c)
-        q_wait(4, dev(1, 1 - k), c)
-        q_wait(6, dev(2, 1 - k), c)
+        q_copy(NEAR2, chip(ahead), None, c, me).wait_recv()
+
+        @pl.when(jnp.logical_not(relays(c)))
+        def _():
+            q_copy(FAR2, chip(2), None, c, me).wait_recv()
 
     lane = lax.broadcasted_iota(jnp.int32, (heads, 128), 1)
     where_t = lax.broadcasted_iota(jnp.int32, (1, sl), 1)
@@ -183,8 +221,8 @@
     def scores(g, par):
         b = g * 2 + par
         slot = (g % PAIRS) * 2 + par
-        qa = qg[:, g, :, pl.ds(par * lat, lat)].reshape(heads, lat)
-        qr = qg[:, g, :, pl.ds(2 * lat, 2 * ROPE)].reshape(heads, 2 * ROPE)
+        qa = qg[:, g, :, :, pl.ds(par * lat, lat)].reshape(heads, lat)
+        qr = qg[:, g, :, :, pl.ds(2 * lat, 2 * ROPE)].reshape(heads, 2 * ROPE)
         s = jnp.dot(qa, cbuf[slot, pl.ds(0, lat), :], preferred_element_type=F32)
         s = s + jnp.dot(qr, cbuf[slot, pl.ds(lat, 2 * ROPE), :], preferred_element_type=F32)
         return jnp.where(where_t < len_ref[b] - base, s * SCALE, -jnp.inf)
@@ -243,9 +281,6 @@
 
     def to_partner(c, kind, src, srcs):
         return o_copies(c, kind, src, srcs, inc.at[kind - MINE, rows(c)], ins.at[kind, c], partner)
-
-    def chip(step):
-        return (x + step + chips) % chips
 
     def sends(c):
         way = sign(c)
@@ -345,8 +380,14 @@
     lax.fori_loop(0, nc + LAG_F, step, 0)
 
     def drain(c, _):
-        for kind in range(7):
-            q_copy(kind, me, c, me).wait_send()
+        for cp in (own(c), own_share(c), partners(c), near_share(c)):
+            cp.wait_send()
+
+        @pl.when(relays(c))
+        def _():
+            passed(c).wait_send()
+            far_share(c).wait_send()
+
         for cp in sends(c) + share(c, VIA) + share(c, DIRECT) + sum_copies(c):
             cp.wait_send()
         return 0
@@ -372,7 +413,7 @@
             scratch_shapes=[
                 pltpu.SMEM((nb,), jnp.int32),
                 pltpu.VMEM((nb, hl, wd), BF16),
-                pltpu.VMEM((n, nb // 2, hl, 2 * wd), BF16),
+                pltpu.VMEM((n // CORES, nb // 2, CORES, hl, 2 * wd), BF16),
                 pltpu.VMEM((n // CORES, nb, CORES, hl, lat), BF16),
                 pltpu.VMEM((n // CORES, nc, CORES, 1, 128), F32),
                 pltpu.VMEM((2, nb, CORES, hl, lat), BF16),

time: 117 us -> 117 us (level)
  no operation moved by 1% of the time
where the time goes in v10:
time: 117 us
  Pallas kernels  116 us (99%)
    pallas_call x1, Pallas kernels, local(): pl.pallas_call(functools.partial(kernel, n), out_shape=pltpu.VMEM((nb, hl...  116 us

profile of v10, /device:TPU:112, one launch (start us, length us, event | category | flops | bytes accessed | tf_op | source)
XLA Modules:
  0.0 116.8 jit_solution(1321363257600185425)
XLA Ops:
  0.0 115.8 %mla_decode.1 = bf16[64,16,512]{2,1,0:T(8,128)(2,1)S(1)} custom-call(s32[64]{0:T(128)} %len_hbm.1, bf16[64,16,576]{2,1,0:T(8,128)(2,1)} %q_ref.1, bf16[64,576,1024]{2,1,0:T(8,128)(2,1)} %bitcast.ct_ref), custom_call_target="tpu_custom_call" | custom-call | tf_op jit(solution)/shard_map/mla_decode/pallas_call | solution.py:408
  115.9 1.0 copy.5

commit v11 on v9

--- a/solution.py
+++ b/solution.py
@@ -23,6 +23,9 @@
 F32 = jnp.float32
 BF16 = jnp.bfloat16
 VIA, DIRECT, MINE, PASS, VIA2, DIRECT2, SUM = range(7)
+FOR_RELAY, FOR_MERGE = 2, 3
+TWO, ONE, TOTAL, ROWS = range(4)
+NEAR, FAR, MATE = range(3)
 
 
 def weights(stats):
@@ -54,8 +57,8 @@
     return jnp.concatenate([w[i * hl:(i + 1) * hl]] * (lat // 128), axis=1) * o.astype(F32)
 
 
-def kernel(n, len_hbm, q_ref, ct_ref, o_ref, len_ref, qraw, qg, od, st, two, twos, inc, ins, lg, rs, rss, cbuf,
-           len_sem, raw_sem, cache_sem, q_send, q_recv, o_send, o_recv, t_send, t_recv):
+def kernel(n, len_hbm, q_ref, ct_ref, o_ref, len_ref, qraw, qg, od, st, two, twos, inc, ins, lg, rs, rss, cbuf, tally,
+           len_sem, raw_sem, cache_sem, q_send, q_recv, o_send, o_recv):
     chips = n // CORES
     nb, hl, wd = q_ref.shape
     lat = wd - ROPE
@@ -73,14 +76,17 @@
     def dev(step, core):
         return ((x + step + chips) % chips) * CORES + core
 
+    def wait_bytes(like, sem):
+        pltpu.make_async_copy(like, like, sem).wait()
+
     def cache_copies(pair, par):
         slot = (pair % PAIRS) * 2 + par
         b = pair * 2 + par
         if par == 0:
-            return [pltpu.make_async_copy(ct_ref.at[b], cbuf.at[slot, pl.ds(0, wd)], cache_sem.at[slot, 0])]
+            return [pltpu.make_async_copy(ct_ref.at[b], cbuf.at[slot, pl.ds(0, wd)], cache_sem.at[slot])]
         return [
-            pltpu.make_async_copy(ct_ref.at[b, pl.ds(0, lat)], cbuf.at[slot, pl.ds(0, lat)], cache_sem.at[slot, 0]),
-            pltpu.make_async_copy(ct_ref.at[b, pl.ds(lat, ROPE)], cbuf.at[slot, pl.ds(wd, ROPE)], cache_sem.at[slot, 1]),
+            pltpu.make_async_copy(ct_ref.at[b, pl.ds(0, lat)], cbuf.at[slot, pl.ds(0, lat)], cache_sem.at[slot]),
+            pltpu.make_async_copy(ct_ref.at[b, pl.ds(lat, ROPE)], cbuf.at[slot, pl.ds(wd, ROPE)], cache_sem.at[slot]),
         ]
 
     def fetch(pair):
@@ -93,12 +99,12 @@
     for peer in peers:
         pl.semaphore_signal(barrier, inc=1, device_id={'dcp': peer}, device_id_type=MESH)
 
-    def raw(c):
-        part = pl.ds(c * CHUNK, CHUNK)
-        return pltpu.make_async_copy(q_ref.at[part], qraw.at[part], raw_sem.at[c])
-
-    for c in range(nc):
-        raw(c).start()
+    def raw(i):
+        part = pl.ds(0, CHUNK) if i == 0 else pl.ds(CHUNK, nb - CHUNK)
+        return pltpu.make_async_copy(q_ref.at[part], qraw.at[part], raw_sem.at[i])
+
+    for i in range(2):
+        raw(i).start()
     lengths = pltpu.make_async_copy(len_hbm, len_ref, len_sem)
     lengths.start()
 
@@ -117,11 +123,11 @@
     def q_copy(kind, src, c, to):
         part = qg.at[src, pl.ds(c * half, half)]
         return pltpu.make_async_remote_copy(
-            src_ref=part, dst_ref=part, send_sem=q_send.at[kind, c], recv_sem=q_recv.at[kind, c],
+            src_ref=part, dst_ref=part, send_sem=q_send, recv_sem=q_recv.at[kind, c],
             device_id={'dcp': to}, device_id_type=MESH)
 
-    def q_wait(kind, src, c):
-        q_copy(kind, src, c, me).wait_recv()
+    def q_wait(kind, count, c):
+        wait_bytes(qg.at[pl.ds(0, count), pl.ds(c * half, half)], q_recv.at[kind, c])
 
     def sign(c):
         return 1 - 2 * (c % 2)
@@ -129,12 +135,15 @@
     def q0(c, _):
         @pl.when(c + 1 < nc)
         def _():
-            raw(c + 1).wait()
+            @pl.when(c == 0)
+            def _():
+                raw(1).wait()
+
             lax.fori_loop((c + 1) * half, (c + 2) * half, pack, 0)
 
-        q_copy(0, me, c, dev(1, k)).start()
-        q_copy(1, me, c, dev(-1, k)).start()
-        q_copy(2, me, c, partner).start()
+        q_copy(NEAR, me, c, dev(1, k)).start()
+        q_copy(NEAR, me, c, dev(-1, k)).start()
+        q_copy(MATE, me, c, partner).start()
         return 0
 
     lax.fori_loop(0, AHEAD, q0, 0)
@@ -146,11 +155,10 @@
 
     def q1(c, _):
         way = -sign(c)
-        q_wait(0, dev(-1, k), c)
-        q_copy(3, dev(-1, k), c, partner).start()
-        q_wait(1, dev(1, k), c)
-        q_copy(4, dev(1, k), c, partner).start()
-        q_copy(5, dev(-way, k), c, dev(way, k)).start()
+        q_wait(NEAR, 2, c)
+        q_copy(FAR, dev(-way, k), c, dev(way, k)).start()
+        q_copy(MATE, dev(-1, k), c, partner).start()
+        q_copy(MATE, dev(1, k), c, partner).start()
 
         @pl.when(c + AHEAD < nc)
         def _():
@@ -162,14 +170,11 @@
     lengths.wait()
 
     def q2(c):
-        q_wait(5, dev(2, k), c)
-        q_copy(6, dev(2, k), c, partner).start()
+        q_wait(FAR, 1, c)
+        q_copy(MATE, dev(2, k), c, partner).start()
 
     def q3(c):
-        q_wait(2, partner, c)
-        q_wait(3, dev(-1, 1 - k), c)
-        q_wait(4, dev(1, 1 - k), c)
-        q_wait(6, dev(2, 1 - k), c)
+        q_wait(MATE, chips, c)
 
     lane = lax.broadcasted_iota(jnp.int32, (heads, 128), 1)
     where_t = lax.broadcasted_iota(jnp.int32, (1, sl), 1)
@@ -177,8 +182,8 @@
 
     def arrive(g):
         for par in range(2):
-            for cp in cache_copies(g, par):
-                cp.wait()
+            slot = (g % PAIRS) * 2 + par
+            wait_bytes(cbuf.at[slot, pl.ds(0, wd)], cache_sem.at[slot])
 
     def scores(g, par):
         b = g * 2 + par
@@ -227,22 +232,29 @@
     def rows(c):
         return pl.ds(c * CHUNK, CHUNK)
 
-    def o_copies(c, kind, src, srcs, dst, dsts, to):
+    row = 128 * 4
+    block = CHUNK * hl * lat * 2 // row
+
+    def o_copies(c, send, recv, src, srcs, dst, dsts, to):
         return [
             pltpu.make_async_remote_copy(
-                src_ref=src, dst_ref=dst, send_sem=o_send.at[kind, c], recv_sem=o_recv.at[kind, c],
+                src_ref=src, dst_ref=dst, send_sem=o_send.at[send], recv_sem=o_recv.at[recv, c],
                 device_id={'dcp': to}, device_id_type=MESH),
             pltpu.make_async_remote_copy(
-                src_ref=srcs, dst_ref=dsts, send_sem=t_send.at[kind, c], recv_sem=t_recv.at[kind, c],
+                src_ref=srcs, dst_ref=dsts, send_sem=o_send.at[ROWS], recv_sem=o_recv.at[recv, c],
                 device_id={'dcp': to}, device_id_type=MESH),
         ]
 
+    def o_wait(c, recv, count):
+        wait_bytes(tally.at[pl.ds(0, count)], o_recv.at[recv, c])
+
     def to_chip(c, kind, head, step):
-        return o_copies(c, kind, od.at[head, rows(c)], st.at[head, c], two.at[kind, rows(c)], twos.at[kind, c],
+        return o_copies(c, TWO, kind, od.at[head, rows(c)], st.at[head, c], two.at[kind, rows(c)], twos.at[kind, c],
                         dev(step, k))
 
     def to_partner(c, kind, src, srcs):
-        return o_copies(c, kind, src, srcs, inc.at[kind - MINE, rows(c)], ins.at[kind, c], partner)
+        recv = FOR_RELAY if kind in (PASS, VIA2) else FOR_MERGE
+        return o_copies(c, ONE, recv, src, srcs, inc.at[kind - MINE, rows(c)], ins.at[kind, c], partner)
 
     def chip(step):
         return (x + step + chips) % chips
@@ -259,21 +271,15 @@
         return to_partner(c, kind + VIA2, two.at[kind, rows(c), 1 - k], twos.at[kind, c, 1 - k])
 
     def pass_on(c, kind):
-        for cp in to_chip(c, kind, x, 0):
-            cp.wait_recv()
+        o_wait(c, kind, 2 * (block + 1))
         for cp in share(c, kind):
             cp.start()
 
-    def partner_wait(c, kind):
-        for cp in to_partner(c, kind, inc.at[kind - MINE, rows(c)], ins.at[kind, c]):
-            cp.wait_recv()
-
     def sum_copies(c):
-        return o_copies(c, SUM, rs.at[rows(c)], rss.at[c], lg.at[rows(c)], ins.at[SUM, c], dev(sign(c), k))
+        return o_copies(c, TOTAL, FOR_MERGE, rs.at[rows(c)], rss.at[c], lg.at[rows(c)], ins.at[SUM, c], dev(sign(c), k))
 
     def relay(c):
-        for kind in (PASS, VIA2):
-            partner_wait(c, kind)
+        o_wait(c, FOR_RELAY, 2 * (block + 1))
         mine = chip(sign(c))
         w, lse = weights([st[mine, c, k], ins[PASS, c], twos[VIA, c, k], ins[VIA2, c]])
         w = [columns(r) for r in w]
@@ -289,10 +295,7 @@
             cp.start()
 
     def merge(c):
-        for kind in (MINE, DIRECT2):
-            partner_wait(c, kind)
-        for cp in sum_copies(c):
-            cp.wait_recv()
+        o_wait(c, FOR_MERGE, 4 * block + 3)
         w, _ = weights([st[x, c, k], ins[MINE, c], twos[DIRECT, c, k], ins[DIRECT2, c], ins[SUM, c]])
         w = [columns(r) for r in w]
         for i in range(CHUNK):
@@ -344,14 +347,11 @@
 
     lax.fori_loop(0, nc + LAG_F, step, 0)
 
-    def drain(c, _):
-        for kind in range(7):
-            q_copy(kind, me, c, me).wait_send()
-        for cp in sends(c) + share(c, VIA) + share(c, DIRECT) + sum_copies(c):
-            cp.wait_send()
-        return 0
-
-    lax.fori_loop(0, nc, drain, 0)
+    wait_bytes(qg.at[pl.ds(0, n - 1)], q_send)
+    wait_bytes(two, o_send.at[TWO])
+    wait_bytes(inc, o_send.at[ONE])
+    wait_bytes(lg, o_send.at[TOTAL])
+    wait_bytes(tally.at[pl.ds(0, nc * (2 * CORES + 5))], o_send.at[ROWS])
 
 
 def solution(mesh):
@@ -383,15 +383,14 @@
                 pltpu.VMEM((nb, hl, lat), F32),
                 pltpu.VMEM((nc, 1, 128), F32),
                 pltpu.VMEM((2 * PAIRS, wd + ROPE, sl), BF16),
+                pltpu.VMEM((4 * CHUNK * hl * lat // 256 + 3, 1, 128), F32),
                 dma,
-                dma((nc,)),
-                dma((2 * PAIRS, 2)),
-                dma((7, nc)),
-                dma((7, nc)),
-                dma((7, nc)),
-                dma((7, nc)),
-                dma((7, nc)),
-                dma((7, nc)),
+                dma((2,)),
+                dma((2 * PAIRS,)),
+                dma,
+                dma((3, nc)),
+                dma((4,)),
+                dma((4, nc)),
             ],
             compiler_params=pltpu.CompilerParams(
                 collective_id=0, has_side_effects=True, vmem_limit_bytes=56 * 1024 * 1024),

time: 117 us -> 114 us (0.974)
  Pallas kernels: 116 us -> 113 us
    pallas_call x1, Pallas kernels: 116 us -> 113 us  [local(): pl.pallas_call(functools.partial(kernel, n), out_shape=pltpu.VMEM((nb, hl...]
where the time goes in v11:
time: 114 us
  Pallas kernels  113 us (99%)
    pallas_call x1, Pallas kernels, local(): pl.pallas_call(functools.partial(kernel, n), out_shape=pltpu.VMEM((nb, hl...  113 us

profile of v11, /device:TPU:112, one launch (start us, length us, event | category | flops | bytes accessed | tf_op | source)
XLA Modules:
  0.0 114.1 jit_solution(4662253999039607979)
XLA Ops:
  0.0 113.1 %mla_decode.1 = bf16[64,16,512]{2,1,0:T(8,128)(2,1)S(1)} custom-call(s32[64]{0:T(128)} %len_hbm.1, bf16[64,16,576]{2,1,0:T(8,128)(2,1)} %q_ref.1, bf16[64,576,1024]{2,1,0:T(8,128)(2,1)} %bitcast.ct_ref), custom_call_target="tpu_custom_call" | custom-call | tf_op jit(solution)/shard_map/mla_decode/pallas_call | solution.py:367
  113.1 1.0 copy.5

commit v12 on v11

--- a/solution.py
+++ b/solution.py
@@ -83,10 +83,10 @@
         slot = (pair % PAIRS) * 2 + par
         b = pair * 2 + par
         if par == 0:
-            return [pltpu.make_async_copy(ct_ref.at[b], cbuf.at[slot, pl.ds(0, wd)], cache_sem.at[slot])]
+            return [pltpu.make_async_copy(ct_ref.at[b], cbuf.at[slot, pl.ds(0, wd)], cache_sem.at[pair % PAIRS])]
         return [
-            pltpu.make_async_copy(ct_ref.at[b, pl.ds(0, lat)], cbuf.at[slot, pl.ds(0, lat)], cache_sem.at[slot]),
-            pltpu.make_async_copy(ct_ref.at[b, pl.ds(lat, ROPE)], cbuf.at[slot, pl.ds(wd, ROPE)], cache_sem.at[slot]),
+            pltpu.make_async_copy(ct_ref.at[b, pl.ds(0, lat)], cbuf.at[slot, pl.ds(0, lat)], cache_sem.at[pair % PAIRS]),
+            pltpu.make_async_copy(ct_ref.at[b, pl.ds(lat, ROPE)], cbuf.at[slot, pl.ds(wd, ROPE)], cache_sem.at[pair % PAIRS]),
         ]
 
     def fetch(pair):
@@ -100,10 +100,10 @@
         pl.semaphore_signal(barrier, inc=1, device_id={'dcp': peer}, device_id_type=MESH)
 
     def raw(i):
-        part = pl.ds(0, CHUNK) if i == 0 else pl.ds(CHUNK, nb - CHUNK)
+        part = pl.ds(i * CHUNK, CHUNK if i < 2 else nb - 2 * CHUNK)
         return pltpu.make_async_copy(q_ref.at[part], qraw.at[part], raw_sem.at[i])
 
-    for i in range(2):
+    for i in range(3):
         raw(i).start()
     lengths = pltpu.make_async_copy(len_hbm, len_ref, len_sem)
     lengths.start()
@@ -135,9 +135,10 @@
     def q0(c, _):
         @pl.when(c + 1 < nc)
         def _():
-            @pl.when(c == 0)
-            def _():
-                raw(1).wait()
+            for i in (1, 2):
+                @pl.when(c == i - 1)
+                def _():
+                    raw(i).wait()
 
             lax.fori_loop((c + 1) * half, (c + 2) * half, pack, 0)
 
@@ -181,9 +182,7 @@
     base = me * sl
 
     def arrive(g):
-        for par in range(2):
-            slot = (g % PAIRS) * 2 + par
-            wait_bytes(cbuf.at[slot, pl.ds(0, wd)], cache_sem.at[slot])
+        wait_bytes(cbuf.at[pl.ds((g % PAIRS) * 2, 2), pl.ds(0, wd)], cache_sem.at[g % PAIRS])
 
     def scores(g, par):
         b = g * 2 + par
@@ -235,18 +234,21 @@
     row = 128 * 4
     block = CHUNK * hl * lat * 2 // row
 
+    def arrived(recv, c):
+        return q_recv.at[{FOR_RELAY: FAR, FOR_MERGE: NEAR}[recv], c] if recv >= FOR_RELAY else o_recv.at[recv, c]
+
     def o_copies(c, send, recv, src, srcs, dst, dsts, to):
         return [
             pltpu.make_async_remote_copy(
-                src_ref=src, dst_ref=dst, send_sem=o_send.at[send], recv_sem=o_recv.at[recv, c],
+                src_ref=src, dst_ref=dst, send_sem=o_send.at[send], recv_sem=arrived(recv, c),
                 device_id={'dcp': to}, device_id_type=MESH),
             pltpu.make_async_remote_copy(
-                src_ref=srcs, dst_ref=dsts, send_sem=o_send.at[ROWS], recv_sem=o_recv.at[recv, c],
+                src_ref=srcs, dst_ref=dsts, send_sem=o_send.at[ROWS], recv_sem=arrived(recv, c),
                 device_id={'dcp': to}, device_id_type=MESH),
         ]
 
     def o_wait(c, recv, count):
-        wait_bytes(tally.at[pl.ds(0, count)], o_recv.at[recv, c])
+        wait_bytes(tally.at[pl.ds(0, count)], arrived(recv, c))
 
     def to_chip(c, kind, head, step):
         return o_copies(c, TWO, kind, od.at[head, rows(c)], st.at[head, c], two.at[kind, rows(c)], twos.at[kind, c],
@@ -385,12 +387,12 @@
                 pltpu.VMEM((2 * PAIRS, wd + ROPE, sl), BF16),
                 pltpu.VMEM((4 * CHUNK * hl * lat // 256 + 3, 1, 128), F32),
                 dma,
-                dma((2,)),
-                dma((2 * PAIRS,)),
+                dma((3,)),
+                dma((PAIRS,)),
                 dma,
                 dma((3, nc)),
                 dma((4,)),
-                dma((4, nc)),
+                dma((2, nc)),
             ],
             compiler_params=pltpu.CompilerParams(
                 collective_id=0, has_side_effects=True, vmem_limit_bytes=56 * 1024 * 1024),

time: 114 us -> 114 us (level)
  no operation moved by 1% of the time
where the time goes in v12:
time: 114 us
  Pallas kernels  113 us (99%)
    pallas_call x1, Pallas kernels, local(): pl.pallas_call(functools.partial(kernel, n), out_shape=pltpu.VMEM((nb, hl...  113 us

profile of v12, /device:TPU:112, one launch (start us, length us, event | category | flops | bytes accessed | tf_op | source)
XLA Modules:
  0.0 113.8 jit_solution(16881368881675191271)
XLA Ops:
  0.0 112.8 %mla_decode.1 = bf16[64,16,512]{2,1,0:T(8,128)(2,1)S(1)} custom-call(s32[64]{0:T(128)} %len_hbm.1, bf16[64,16,576]{2,1,0:T(8,128)(2,1)} %q_ref.1, bf16[64,576,1024]{2,1,0:T(8,128)(2,1)} %bitcast.ct_ref), custom_call_target="tpu_custom_call" | custom-call | tf_op jit(solution)/shard_map/mla_decode/pallas_call | solution.py:369
  112.8 1.0 copy.5

commit v13 on v12

--- a/solution.py
+++ b/solution.py
@@ -16,7 +16,6 @@
 LEAD = 3
 LAG_V = 2
 LAG_R = 3
-LAG_D = 4
 LAG_F = 6
 
 MESH = pl.DeviceIdType.MESH
@@ -58,7 +57,7 @@
 
 
 def kernel(n, len_hbm, q_ref, ct_ref, o_ref, len_ref, qraw, qg, od, st, two, twos, inc, ins, lg, rs, rss, cbuf, tally,
-           len_sem, raw_sem, cache_sem, q_send, q_recv, o_send, o_recv):
+           cache_sem, q_send, q_recv, mate_recv, o_send, o_recv):
     chips = n // CORES
     nb, hl, wd = q_ref.shape
     lat = wd - ROPE
@@ -94,19 +93,19 @@
             for cp in cache_copies(pair, par):
                 cp.start()
 
+    def raw(i):
+        part = pl.ds(i * CHUNK, CHUNK if i < 2 else nb - 2 * CHUNK)
+        return pltpu.make_async_copy(q_ref.at[part], qraw.at[part], cache_sem.at[i])
+
+    for i in range(3):
+        raw(i).start()
+    lengths = pltpu.make_async_copy(len_hbm, len_ref, cache_sem.at[3])
+    lengths.start()
+
     barrier = pltpu.get_barrier_semaphore()
     peers = [dev(1, k), dev(-1, k), partner]
     for peer in peers:
         pl.semaphore_signal(barrier, inc=1, device_id={'dcp': peer}, device_id_type=MESH)
-
-    def raw(i):
-        part = pl.ds(i * CHUNK, CHUNK if i < 2 else nb - 2 * CHUNK)
-        return pltpu.make_async_copy(q_ref.at[part], qraw.at[part], raw_sem.at[i])
-
-    for i in range(3):
-        raw(i).start()
-    lengths = pltpu.make_async_copy(len_hbm, len_ref, len_sem)
-    lengths.start()
 
     def pack(g, _):
         for par in range(2):
@@ -123,7 +122,7 @@
     def q_copy(kind, src, c, to):
         part = qg.at[src, pl.ds(c * half, half)]
         return pltpu.make_async_remote_copy(
-            src_ref=part, dst_ref=part, send_sem=q_send, recv_sem=q_recv.at[kind, c],
+            src_ref=part, dst_ref=part, send_sem=q_send, recv_sem=mate_recv.at[c // 2] if kind == MATE else q_recv.at[kind, c],
             device_id={'dcp': to}, device_id_type=MESH)
 
     def q_wait(kind, count, c):
@@ -149,6 +148,7 @@
 
     lax.fori_loop(0, AHEAD, q0, 0)
 
+    lengths.wait()
     for g in range(PAIRS):
         fetch(g)
         cbuf[2 * g, pl.ds(wd, ROPE), :] = jnp.zeros((ROPE, sl), BF16)
@@ -168,14 +168,15 @@
         return 0
 
     lax.fori_loop(0, LEAD, q1, 0)
-    lengths.wait()
 
     def q2(c):
         q_wait(FAR, 1, c)
         q_copy(MATE, dev(2, k), c, partner).start()
 
     def q3(c):
-        q_wait(MATE, chips, c)
+        @pl.when(c % 2 == 0)
+        def _():
+            wait_bytes(qg.at[pl.ds(0, chips), pl.ds(c * half, 2 * half)], mate_recv.at[c // 2])
 
     lane = lax.broadcasted_iota(jnp.int32, (heads, 128), 1)
     where_t = lax.broadcasted_iota(jnp.int32, (1, sl), 1)
@@ -235,7 +236,7 @@
     block = CHUNK * hl * lat * 2 // row
 
     def arrived(recv, c):
-        return q_recv.at[{FOR_RELAY: FAR, FOR_MERGE: NEAR}[recv], c] if recv >= FOR_RELAY else o_recv.at[recv, c]
+        return q_recv.at[{FOR_RELAY: FAR, FOR_MERGE: NEAR}[recv], c] if recv >= FOR_RELAY else o_recv.at[c]
 
     def o_copies(c, send, recv, src, srcs, dst, dsts, to):
         return [
@@ -272,9 +273,9 @@
     def share(c, kind):
         return to_partner(c, kind + VIA2, two.at[kind, rows(c), 1 - k], twos.at[kind, c, 1 - k])
 
-    def pass_on(c, kind):
-        o_wait(c, kind, 2 * (block + 1))
-        for cp in share(c, kind):
+    def pass_on(c):
+        o_wait(c, VIA, 4 * (block + 1))
+        for cp in share(c, VIA) + share(c, DIRECT):
             cp.start()
 
     def sum_copies(c):
@@ -331,15 +332,11 @@
 
         @pl.when(jnp.logical_and(t >= LAG_V, t < nc + LAG_V))
         def _():
-            pass_on(t - LAG_V, VIA)
+            pass_on(t - LAG_V)
 
         @pl.when(jnp.logical_and(t >= LAG_R, t < nc + LAG_R))
         def _():
             relay(t - LAG_R)
-
-        @pl.when(jnp.logical_and(t >= LAG_D, t < nc + LAG_D))
-        def _():
-            pass_on(t - LAG_D, DIRECT)
 
         @pl.when(t >= LAG_F)
         def _():
@@ -385,14 +382,13 @@
                 pltpu.VMEM((nb, hl, lat), F32),
                 pltpu.VMEM((nc, 1, 128), F32),
                 pltpu.VMEM((2 * PAIRS, wd + ROPE, sl), BF16),
-                pltpu.VMEM((4 * CHUNK * hl * lat // 256 + 3, 1, 128), F32),
-                dma,
-                dma((3,)),
+                pltpu.VMEM((4 * CHUNK * hl * lat // 256 + 4, 1, 128), F32),
                 dma((PAIRS,)),
                 dma,
-                dma((3, nc)),
+                dma((2, nc)),
+                dma((nc // 2,)),
                 dma((4,)),
-                dma((2, nc)),
+                dma((nc,)),
             ],
             compiler_params=pltpu.CompilerParams(
                 collective_id=0, has_side_effects=True, vmem_limit_bytes=56 * 1024 * 1024),

time: 114 us -> 114 us (level)
  no operation moved by 1% of the time
where the time goes in v13:
time: 114 us
  Pallas kernels  113 us (99%)
    pallas_call x1, Pallas kernels, local(): pl.pallas_call(functools.partial(kernel, n), out_shape=pltpu.VMEM((nb, hl...  113 us

profile of v13, /device:TPU:112, one launch (start us, length us, event | category | flops | bytes accessed | tf_op | source)
XLA Modules:
  0.0 113.6 jit_solution(450805861546397945)
XLA Ops:
  0.0 112.6 %mla_decode.1 = bf16[64,16,512]{2,1,0:T(8,128)(2,1)S(1)} custom-call(s32[64]{0:T(128)} %len_hbm.1, bf16[64,16,576]{2,1,0:T(8,128)(2,1)} %q_ref.1, bf16[64,576,1024]{2,1,0:T(8,128)(2,1)} %bitcast.ct_ref), custom_call_target="tpu_custom_call" | custom-call | tf_op jit(solution)/shard_map/mla_decode/pallas_call | solution.py:366
  112.6 1.0 copy.5

commit v14 on v13

--- a/solution.py
+++ b/solution.py
@@ -24,7 +24,7 @@
 VIA, DIRECT, MINE, PASS, VIA2, DIRECT2, SUM = range(7)
 FOR_RELAY, FOR_MERGE = 2, 3
 TWO, ONE, TOTAL, ROWS = range(4)
-NEAR, FAR, MATE = range(3)
+NEAR, FAR, MATE, OWN = range(4)
 
 
 def weights(stats):
@@ -103,7 +103,7 @@
     lengths.start()
 
     barrier = pltpu.get_barrier_semaphore()
-    peers = [dev(1, k), dev(-1, k), partner]
+    peers = [dev(1, 0), dev(1, 1), dev(-1, 0), dev(-1, 1), partner]
     for peer in peers:
         pl.semaphore_signal(barrier, inc=1, device_id={'dcp': peer}, device_id_type=MESH)
 
@@ -122,8 +122,13 @@
     def q_copy(kind, src, c, to):
         part = qg.at[src, pl.ds(c * half, half)]
         return pltpu.make_async_remote_copy(
-            src_ref=part, dst_ref=part, send_sem=q_send, recv_sem=mate_recv.at[c // 2] if kind == MATE else q_recv.at[kind, c],
+            src_ref=part, dst_ref=part, send_sem=q_send.at[c // (nc - 1)], recv_sem=q_arrived(kind, c),
             device_id={'dcp': to}, device_id_type=MESH)
+
+    def q_arrived(kind, c):
+        if kind == OWN:
+            return mate_recv.at[c // 2 + c // (nc - 1)]
+        return mate_recv.at[c // 2] if kind == MATE else q_recv.at[kind, c]
 
     def q_wait(kind, count, c):
         wait_bytes(qg.at[pl.ds(0, count), pl.ds(c * half, half)], q_recv.at[kind, c])
@@ -141,9 +146,22 @@
 
             lax.fori_loop((c + 1) * half, (c + 2) * half, pack, 0)
 
-        q_copy(NEAR, me, c, dev(1, k)).start()
-        q_copy(NEAR, me, c, dev(-1, k)).start()
-        q_copy(MATE, me, c, partner).start()
+        @pl.when(jnp.logical_or(c < nc - 1, k == 1))
+        def _():
+            q_copy(NEAR, me, c, dev(1, k)).start()
+            q_copy(NEAR, me, c, dev(-1, k)).start()
+
+        q_copy(OWN, me, c, partner).start()
+
+        @pl.when(c == nc - 1)
+        def _():
+            wait_bytes(qg.at[0, pl.ds(c * half, half)], q_arrived(OWN, nc - 1))
+
+            @pl.when(k == 1)
+            def _():
+                q_copy(NEAR, partner, c, dev(1, 0)).start()
+                q_copy(NEAR, partner, c, dev(-1, 0)).start()
+
         return 0
 
     lax.fori_loop(0, AHEAD, q0, 0)
@@ -174,9 +192,13 @@
         q_copy(MATE, dev(2, k), c, partner).start()
 
     def q3(c):
-        @pl.when(c % 2 == 0)
+        @pl.when(jnp.logical_and(c % 2 == 0, c < nc - 2))
         def _():
             wait_bytes(qg.at[pl.ds(0, chips), pl.ds(c * half, 2 * half)], mate_recv.at[c // 2])
+
+        @pl.when(c == nc - 2)
+        def _():
+            wait_bytes(qg.at[pl.ds(0, 2 * chips - 1), pl.ds(c * half, half)], mate_recv.at[c // 2])
 
     lane = lax.broadcasted_iota(jnp.int32, (heads, 128), 1)
     where_t = lax.broadcasted_iota(jnp.int32, (1, sl), 1)
@@ -346,7 +368,16 @@
 
     lax.fori_loop(0, nc + LAG_F, step, 0)
 
-    wait_bytes(qg.at[pl.ds(0, n - 1)], q_send)
+    wait_bytes(qg.at[pl.ds(0, 7), pl.ds(0, (nc - 1) * half)], q_send.at[0])
+
+    @pl.when(k == 0)
+    def _():
+        wait_bytes(qg.at[pl.ds(0, 5), pl.ds(0, half)], q_send.at[1])
+
+    @pl.when(k == 1)
+    def _():
+        wait_bytes(qg.at[pl.ds(0, 3), pl.ds(0, 3 * half)], q_send.at[1])
+
     wait_bytes(two, o_send.at[TWO])
     wait_bytes(inc, o_send.at[ONE])
     wait_bytes(lg, o_send.at[TOTAL])
@@ -384,9 +415,9 @@
                 pltpu.VMEM((2 * PAIRS, wd + ROPE, sl), BF16),
                 pltpu.VMEM((4 * CHUNK * hl * lat // 256 + 4, 1, 128), F32),
                 dma((PAIRS,)),
-                dma,
+                dma((2,)),
                 dma((2, nc)),
-                dma((nc // 2,)),
+                dma((nc // 2 + 1,)),
                 dma((4,)),
                 dma((nc,)),
             ],

time: 114 us -> 114 us (level)
  no operation moved by 1% of the time
where the time goes in v14:
time: 114 us; the launch traced here: 113 us
  Pallas kernels  112 us (98%)
    pallas_call x1, Pallas kernels, local(): pl.pallas_call(functools.partial(kernel, n), out_shape=pltpu.VMEM((nb, hl...  112 us

profile of v14, /device:TPU:112, one launch (start us, length us, event | category | flops | bytes accessed | tf_op | source)
XLA Modules:
  0.0 113.0 jit_solution(12653145039277686994)
XLA Ops:
  0.0 112.0 %mla_decode.1 = bf16[64,16,512]{2,1,0:T(8,128)(2,1)S(1)} custom-call(s32[64]{0:T(128)} %len_hbm.1, bf16[64,16,576]{2,1,0:T(8,128)(2,1)} %q_ref.1, bf16[64,576,1024]{2,1,0:T(8,128)(2,1)} %bitcast.ct_ref), custom_call_target="tpu_custom_call" | custom-call | tf_op jit(solution)/shard_map/mla_decode/pallas_call | solution.py:397
  112.0 1.0 copy.5

commit v15 on v14

--- a/solution.py
+++ b/solution.py
@@ -119,8 +119,8 @@
     lax.fori_loop(0, half, pack, 0)
     pl.semaphore_wait(barrier, len(peers))
 
-    def q_copy(kind, src, c, to):
-        part = qg.at[src, pl.ds(c * half, half)]
+    def q_copy(kind, src, c, to, skip=0, count=half):
+        part = qg.at[src, pl.ds(c * half + skip, count)]
         return pltpu.make_async_remote_copy(
             src_ref=part, dst_ref=part, send_sem=q_send.at[c // (nc - 1)], recv_sem=q_arrived(kind, c),
             device_id={'dcp': to}, device_id_type=MESH)
@@ -151,6 +151,11 @@
             q_copy(NEAR, me, c, dev(1, k)).start()
             q_copy(NEAR, me, c, dev(-1, k)).start()
 
+        @pl.when(jnp.logical_and(c == nc - 1, k == 0))
+        def _():
+            q_copy(NEAR, me, c, dev(1, 0), 0, half // 2).start()
+            q_copy(NEAR, me, c, dev(-1, 0), 0, half // 2).start()
+
         q_copy(OWN, me, c, partner).start()
 
         @pl.when(c == nc - 1)
@@ -159,8 +164,8 @@
 
             @pl.when(k == 1)
             def _():
-                q_copy(NEAR, partner, c, dev(1, 0)).start()
-                q_copy(NEAR, partner, c, dev(-1, 0)).start()
+                q_copy(NEAR, partner, c, dev(1, 0), half // 2, half // 2).start()
+                q_copy(NEAR, partner, c, dev(-1, 0), half // 2, half // 2).start()
 
         return 0
 
@@ -372,11 +377,11 @@
 
     @pl.when(k == 0)
     def _():
-        wait_bytes(qg.at[pl.ds(0, 5), pl.ds(0, half)], q_send.at[1])
+        wait_bytes(qg.at[pl.ds(0, 6), pl.ds(0, half)], q_send.at[1])
 
     @pl.when(k == 1)
     def _():
-        wait_bytes(qg.at[pl.ds(0, 3), pl.ds(0, 3 * half)], q_send.at[1])
+        wait_bytes(qg.at[pl.ds(0, 8), pl.ds(0, half)], q_send.at[1])
 
     wait_bytes(two, o_send.at[TWO])
     wait_bytes(inc, o_send.at[ONE])

time: 114 us -> 114 us (level)
  no operation moved by 1% of the time
where the time goes in v15:
time: 114 us; the launch traced here: 113 us
  Pallas kernels  112 us (98%)
    pallas_call x1, Pallas kernels, local(): pl.pallas_call(functools.partial(kernel, n), out_shape=pltpu.VMEM((nb, hl...  112 us

profile of v15, /device:TPU:112, one launch (start us, length us, event | category | flops | bytes accessed | tf_op | source)
XLA Modules:
  0.0 112.8 jit_solution(11074504231567357380)
XLA Ops:
  0.0 111.9 %mla_decode.1 = bf16[64,16,512]{2,1,0:T(8,128)(2,1)S(1)} custom-call(s32[64]{0:T(128)} %len_hbm.1, bf16[64,16,576]{2,1,0:T(8,128)(2,1)} %q_ref.1, bf16[64,576,1024]{2,1,0:T(8,128)(2,1)} %bitcast.ct_ref), custom_call_target="tpu_custom_call" | custom-call | tf_op jit(solution)/shard_map/mla_decode/pallas_call | solution.py:402
  111.9 1.0 copy.5

commit v16 on v13

--- a/solution.py
+++ b/solution.py
@@ -132,18 +132,20 @@
         return 1 - 2 * (c % 2)
 
     def q0(c, _):
-        @pl.when(c + 1 < nc)
-        def _():
-            for i in (1, 2):
-                @pl.when(c == i - 1)
-                def _():
-                    raw(i).wait()
-
-            lax.fori_loop((c + 1) * half, (c + 2) * half, pack, 0)
-
         q_copy(NEAR, me, c, dev(1, k)).start()
         q_copy(NEAR, me, c, dev(-1, k)).start()
         q_copy(MATE, me, c, partner).start()
+
+        @pl.when(c == 0)
+        def _():
+            raw(1).wait()
+            raw(2).wait()
+            lax.fori_loop(half, 3 * half, pack, 0)
+
+        @pl.when(jnp.logical_and(c > 0, c + 2 < nc))
+        def _():
+            lax.fori_loop((c + 2) * half, (c + 3) * half, pack, 0)
+
         return 0
 
     lax.fori_loop(0, AHEAD, q0, 0)

time: 114 us -> 113 us (level)
  no operation moved by 1% of the time
where the time goes in v16:
time: 113 us
  Pallas kernels  112 us (99%)
    pallas_call x1, Pallas kernels, local(): pl.pallas_call(functools.partial(kernel, n), out_shape=pltpu.VMEM((nb, hl...  112 us

profile of v16, /device:TPU:112, one launch (start us, length us, event | category | flops | bytes accessed | tf_op | source)
XLA Modules:
  0.0 113.3 jit_solution(8328963720889162987)
XLA Ops:
  0.0 112.4 %mla_decode.1 = bf16[64,16,512]{2,1,0:T(8,128)(2,1)S(1)} custom-call(s32[64]{0:T(128)} %len_hbm.1, bf16[64,16,576]{2,1,0:T(8,128)(2,1)} %q_ref.1, bf16[64,576,1024]{2,1,0:T(8,128)(2,1)} %bitcast.ct_ref), custom_call_target="tpu_custom_call" | custom-call | tf_op jit(solution)/shard_map/mla_decode/pallas_call | solution.py:368
  112.4 1.0 copy.5
